TPU v7x, 32 devices: a whole 2x2x4 slice. The times are simulated.
32 devices in a mesh: groups: 2 (over x), wide: 16 (over z, y, core).
Axes of the slice: x: 2, y: 2, z: 4, core: 2. Of those that a mesh axis runs over, the one named last changes fastest.
Arguments:
- queries: bfloat16 [256, 3072], P(('groups', 'wide')), parts along dimension 0, may hold values from -15 to 15
- hidden_in: bfloat16 [256, 3072], P(('groups', 'wide')), parts along dimension 0, may hold values from -170 to 170
- prefix_keys: bfloat16 [16384, 512], P(('groups', 'wide')), parts along dimension 0, may hold values from -12 to 12
- prefix_values: bfloat16 [16384, 512], P(('groups', 'wide')), parts along dimension 0, may hold values from -24 to 24
- suffix_keys: bfloat16 [256, 64, 512], P(('groups', 'wide')), parts along dimension 0, may hold values from -21 to 21
- suffix_values: bfloat16 [256, 64, 512], P(('groups', 'wide')), parts along dimension 0, may hold values from -24 to 24
- suffix_length: int32 [256], P(('groups', 'wide')), parts along dimension 0, may hold values from 2 to 64, as said below
- prefix_of: int32 [256, 1], P('groups'), parts along dimension 0, may hold values from 0 to 7; in each aligned block of 8 rows (0 to 7, 8 to 15, ...) at most 2 rows name the same one
- expert_index: int32 [256, 2], P('groups'), parts along dimension 0, may hold values from 0 to 3, all different within a row; in each aligned block of 8 rows (0 to 7, 8 to 15, ...) at most 6 rows name the same one
- gate_logits: float32 [256, 2], P('groups'), parts along dimension 0, may hold values from -6 to 6
- norm_gain: float32 [3072], replicated, may hold values from 0.1 to 1.9
- gate_weight: bfloat16 [3072, 32768], P(None, 'wide'), may hold values from -0.109375 to 0.109375
- up_weight: bfloat16 [3072, 32768], P(None, 'wide'), may hold values from -0.109375 to 0.109375
- down_weight: bfloat16 [32768, 3072], P('wide'), may hold values from -0.125 to 0.125
Outputs:
- attended: bfloat16 [256, 3072], P(('groups', 'wide')), parts along dimension 0
- expert_mix: bfloat16 [256, 3072], P(('groups', 'wide')), parts along dimension 0
There are 2 independent parts, one for each index of `groups`. A program takes and returns all parts, laid end to end along the dimension named above; an argument that names none is the same for every part. Nothing has to cross between parts.
Inputs may be any that keep to these rules, and one draw needn't show every extreme that they name: `prefix_of`: among the requests of one device at most 2 share a prefix; in some of the aligned blocks exactly 2 do. `expert_index`: each request names 2 different experts; among the requests of one device at most 6 name the same expert, and in some aligned blocks exactly 6 do. `suffix_length`: every device holds a request with 64 live suffix tokens.
All inputs are finite; a program needn't handle non-finite values.
Results may differ from a plain program's by a relative error of at most 0.0095.
Values may be sent and summed in bfloat16 or wider, within the bound.
No kernel may reach another device: no remote copies, remote signals or barrier semaphores. Data moves between devices by JAX's collectives and lax.ppermute only.
A program may use at most 128 MiB of HBM per device.

v0:
```python
import math

import jax
import jax.numpy as jnp
from jax import lax
from jax.sharding import PartitionSpec as P

D = 3072
HQ = 24
HK = 4
DH = 128
EXPERTS = 4
PREFIXES = 8
CAPP = 2


masked_score = -1e30


def prefix_part(query_rows, key_rows, value_rows):
    row_count = query_rows.shape[0]
    query_heads = query_rows.reshape(row_count, HK, HQ // HK, DH)
    key_heads = key_rows.reshape(key_rows.shape[0], HK, DH)
    value_heads = value_rows.reshape(value_rows.shape[0], HK, DH)
    scores = jnp.einsum(
        "nkgd,pkd->nkgp", query_heads, key_heads, preferred_element_type=jnp.float32
    ) * (1.0 / math.sqrt(DH))
    block_max = jnp.max(scores, axis=-1)
    weights = jnp.exp(scores - block_max[..., None]).astype(jnp.bfloat16)
    block_sum = jnp.sum(weights.astype(jnp.float32), axis=-1)
    block_out = jnp.einsum(
        "nkgp,pkd->nkgd", weights, value_heads, preferred_element_type=jnp.float32
    )
    return (
        block_out.reshape(row_count, D),
        block_max.reshape(row_count, HQ),
        block_sum.reshape(row_count, HQ),
    )


def suffix_part(query_rows, key_rows, value_rows, lengths):
    row_count = query_rows.shape[0]
    slots_max = key_rows.shape[1]
    query_heads = query_rows.reshape(row_count, HK, HQ // HK, DH)
    key_heads = key_rows.reshape(row_count, slots_max, HK, DH)
    value_heads = value_rows.reshape(row_count, slots_max, HK, DH)
    scores = jnp.einsum(
        "nkgd,nskd->nkgs", query_heads, key_heads, preferred_element_type=jnp.float32
    ) * (1.0 / math.sqrt(DH))
    usable = jnp.arange(slots_max)[None, :] < lengths[:, None]
    scores = jnp.where(usable[:, None, None, :], scores, masked_score)
    block_max = jnp.max(scores, axis=-1)
    weights = jnp.exp(scores - block_max[..., None]).astype(jnp.bfloat16)
    block_sum = jnp.sum(weights.astype(jnp.float32), axis=-1)
    block_out = jnp.einsum(
        "nkgs,nskd->nkgd", weights, value_heads, preferred_element_type=jnp.float32
    )
    return (
        block_out.reshape(row_count, HQ, DH),
        block_max.reshape(row_count, HQ),
        block_sum.reshape(row_count, HQ),
    )


def slot_table(owned_keys, device_key, capacity):
    entries = owned_keys.shape[0]
    alike_key = owned_keys[:, None] == owned_keys[None, :]
    position = jnp.arange(entries)
    earlier = position[None, :] < position[:, None]
    slot_rank = jnp.sum(alike_key & earlier, axis=1)
    matches = device_key[:, None, None] == owned_keys[None, None, :]
    placed = slot_rank[None, None, :] == jnp.arange(capacity)[None, :, None]
    return matches & placed


def merge_parts(part_out, part_max, part_sum, selection, suffix_out, suffix_max, suffix_sum):
    sources, slot_count = (part_max.shape[0], part_max.shape[1])
    masked = jnp.where(selection[..., None], part_max[:, :, None, :], masked_score)
    overall = jnp.maximum(jnp.max(masked, axis=(0, 1)), suffix_max)
    factor = jnp.where(selection[..., None], jnp.exp(masked - overall[None, None]), 0.0)
    out_heads = part_out.reshape(sources, slot_count, HQ, DH)
    suffix_factor = jnp.exp(suffix_max - overall)
    numerator = (
        jnp.einsum("scnh,schd->nhd", factor, out_heads, precision=lax.Precision.HIGHEST)
        + suffix_factor[..., None] * suffix_out
    )
    denominator = (
        jnp.einsum("scnh,sch->nh", factor, part_sum, precision=lax.Precision.HIGHEST)
        + suffix_factor * suffix_sum
    )
    return (numerator / denominator[..., None]).reshape(suffix_out.shape[0], D).astype(jnp.bfloat16)


def local(
    queries,
    hidden_in,
    prefix_keys,
    prefix_values,
    suffix_keys,
    suffix_values,
    suffix_length,
    prefix_of,
    expert_index,
    gate_logits,
    norm_gain,
    gate_weight,
    up_weight,
    down_weight,
):
    devices = lax.axis_size("wide")
    rank_here = lax.axis_index("wide")
    local_rows = queries.shape[0]
    holders_prefix = devices // PREFIXES
    holders_expert = devices // EXPERTS
    start_row = rank_here * local_rows
    suffix_out, suffix_max, suffix_sum = suffix_part(
        queries, suffix_keys, suffix_values, suffix_length
    )
    own_prefix = lax.dynamic_slice_in_dim(prefix_of[:, 0], start_row, local_rows, 0)
    selection = slot_table(own_prefix, jnp.arange(devices) // holders_prefix, CAPP)
    outgoing = jnp.einsum(
        "sci,id->scd", selection.astype(jnp.bfloat16), queries, preferred_element_type=jnp.float32
    ).astype(jnp.bfloat16)
    received = lax.all_to_all(outgoing, "wide", split_axis=0, concat_axis=0, tiled=True)
    slot_count = received.shape[1]
    flattened = received.reshape(devices * slot_count, D)
    part_out, part_max, part_sum = prefix_part(flattened, prefix_keys, prefix_values)
    back_out = lax.all_to_all(
        part_out.reshape(devices, slot_count, D), "wide", split_axis=0, concat_axis=0, tiled=True
    )
    back_max = lax.all_to_all(
        part_max.reshape(devices, slot_count, HQ), "wide", split_axis=0, concat_axis=0, tiled=True
    )
    back_sum = lax.all_to_all(
        part_sum.reshape(devices, slot_count, HQ), "wide", split_axis=0, concat_axis=0, tiled=True
    )
    attended = merge_parts(
        back_out, back_max, back_sum, selection, suffix_out, suffix_max, suffix_sum
    )
    stream = hidden_in.astype(jnp.float32) + attended.astype(jnp.float32)
    normed = (
        stream * lax.rsqrt(jnp.mean(stream * stream, axis=-1, keepdims=True) + 1e-05) * norm_gain
    ).astype(jnp.bfloat16)
    gates = jax.nn.softmax(gate_logits, axis=-1)
    my_expert = rank_here // holders_expert
    share = jnp.sum(gates * (expert_index == my_expert).astype(jnp.float32), axis=1)
    piece = lax.all_gather(normed, "wide", axis=0, tiled=True)
    gate_part = jnp.dot(piece, gate_weight, preferred_element_type=jnp.float32)
    up_part = jnp.dot(piece, up_weight, preferred_element_type=jnp.float32)
    hidden_all = (jax.nn.silu(gate_part) * up_part).astype(jnp.bfloat16)
    mixture = lax.psum_scatter(
        share[:, None] * jnp.dot(hidden_all, down_weight, preferred_element_type=jnp.float32),
        "wide",
        scatter_dimension=0,
        tiled=True,
    )
    return (attended, mixture.astype(jnp.bfloat16))


def solution(mesh):
    placed = (
        P(("groups", "wide"), None),
        P(("groups", "wide"), None),
        P(("groups", "wide"), None),
        P(("groups", "wide"), None),
        P(("groups", "wide"), None, None),
        P(("groups", "wide"), None, None),
        P(("groups", "wide")),
        P("groups", None),
        P("groups", None),
        P("groups", None),
        P(),
        P(None, "wide"),
        P(None, "wide"),
        P("wide", None),
    )
    return jax.shard_map(
        local,
        mesh=mesh,
        in_specs=placed,
        out_specs=(P(("groups", "wide"), None), P(("groups", "wide"), None)),
        check_vma=False,
    )
```

profile of v0, /device:TPU:0, one launch (start us, length us, event | category | flops | bytes accessed | tf_op | source)
XLA Modules:
  0.0 171.0 jit_solution(12314746166808616093)
XLA Ops:
  7.2 0.8 dynamic-slice_bitcast_fusion
  8.0 0.2 convert_reduce_fusion.2
  8.3 1.2 convolution_convert_fusion
  9.5 0.9 copy.75
  10.4 7.4 %all-to-all-start = ((bf16[16,2,3072]{2,1,0:T(2,128)(2,1)}), bf16[16,2,3072]{2,1,0:T(2,128)(2,1)S(1)}, u32[]{:S(2)}, u32[]{:S(2)}) async-start(bf16[16,2,3072]{2,1,0:T(2,128)(2,1)} %copy.75), calls=%async_computation | async-start | bytes 393216 | tf_op jit(solution)/shard_map/all_to_all | solution.py:124
  17.8 0.1 broadcast_and_fusion
  17.9 0.7 reduce_max.39
  18.6 0.7 fusion.34
  19.3 0.7 iota_compare_fusion
  20.0 1.2 reshape.161
  21.2 0.1 reshape.162
  21.3 0.5 fusion.38
  21.8 0.2 convert_reduce_fusion.1
  22.0 1.0 fusion.8
  23.0 3.7 %all-to-all-done = bf16[16,2,3072]{2,1,0:T(2,128)(2,1)S(1)} async-done(((bf16[16,2,3072]{2,1,0:T(2,128)(2,1)}), bf16[16,2,3072]{2,1,0:T(2,128)(2,1)S(1)}, u32[]{:S(2)}, u32[]{:S(2)}) %all-to-all-start) | async-done | bytes 196640 | tf_op jit(solution)/shard_map/all_to_all | solution.py:124
  26.7 0.2 reshape_reshape.12
  26.9 0.5 bitcast_reduce_fusion
  27.4 0.1 copy.81
  27.5 0.7 reshape_reshape.14
  28.2 3.5 %all-to-all-start.2 = ((f32[16,2,24]{2,1,0:T(2,128)}), f32[16,2,24]{2,1,0:T(2,128)S(1)}, u32[]{:S(2)}, u32[]{:S(2)}) async-start(f32[16,2,24]{2,1,0:T(2,128)} %reshape_reshape.14), calls=%async_computation.2 | async-start | bytes 32768 | tf_op jit(solution)/shard_map/all_to_all | solution.py:131
  31.7 0.5 convert_reduce_fusion
  32.2 0.1 copy.91
  32.3 0.7 reshape_reshape.15
  33.1 5.1 %all-to-all-done.2 = f32[16,2,24]{2,1,0:T(2,128)S(1)} async-done(((f32[16,2,24]{2,1,0:T(2,128)}), f32[16,2,24]{2,1,0:T(2,128)S(1)}, u32[]{:S(2)}, u32[]{:S(2)}) %all-to-all-start.2) | async-done | bytes 3104 | tf_op jit(solution)/shard_map/all_to_all | solution.py:131
  38.2 3.5 %all-to-all-start.3 = ((f32[16,2,24]{2,1,0:T(2,128)}), f32[16,2,24]{2,1,0:T(2,128)S(1)}, u32[]{:S(2)}, u32[]{:S(2)}) async-start(f32[16,2,24]{2,1,0:T(2,128)} %reshape_reshape.15), calls=%async_computation.3 | async-start | bytes 32768 | tf_op jit(solution)/shard_map/all_to_all | solution.py:134
  41.7 0.4 convolution_bitcast_fusion
  42.2 0.2 copy.79
  42.4 1.0 reshape_reshape.13
  43.4 4.8 %all-to-all-done.3 = f32[16,2,24]{2,1,0:T(2,128)S(1)} async-done(((f32[16,2,24]{2,1,0:T(2,128)}), f32[16,2,24]{2,1,0:T(2,128)S(1)}, u32[]{:S(2)}, u32[]{:S(2)}) %all-to-all-start.3) | async-done | bytes 3104 | tf_op jit(solution)/shard_map/all_to_all | solution.py:134
  48.1 3.6 %all-to-all-start.1 = ((f32[16,2,3072]{2,1,0:T(2,128)}), f32[16,2,3072]{2,1,0:T(2,128)S(1)}, u32[]{:S(2)}, u32[]{:S(2)}) async-start(f32[16,2,3072]{2,1,0:T(2,128)} %reshape_reshape.13), calls=%async_computation.1 | async-start | bytes 786432 | tf_op jit(solution)/shard_map/all_to_all | solution.py:128
  51.8 0.1 reshape.166
  51.9 0.1 reshape.169
  52.0 0.1 copy.82
  52.1 0.1 select_reduce_fusion
  52.3 0.1 copy.86
  52.4 0.1 copy.108
  52.5 0.2 fusion.23
  52.7 0.1 copy.92
  52.9 0.1 bitcast_multiply_fusion
  53.0 10.8 %all-to-all-done.1 = f32[16,2,3072]{2,1,0:T(2,128)S(1)} async-done(((f32[16,2,3072]{2,1,0:T(2,128)}), f32[16,2,3072]{2,1,0:T(2,128)S(1)}, u32[]{:S(2)}, u32[]{:S(2)}) %all-to-all-start.1) | async-done | bytes 393248 | tf_op jit(solution)/shard_map/all_to_all | solution.py:128
  63.8 0.3 reshape.176
  64.2 0.8 multiply_reduce_fusion
  65.0 0.1 multiply_convert_fusion
  65.0 21.3 %all_gather.3 = bf16[128,3072]{1,0:T(8,128)(2,1)S(1)} all-gather(bf16[8,3072]{1,0:T(8,128)(2,1)S(1)} %multiply_convert_fusion), channel_id=1, replica_groups=mesh['groups'=2,'wide'=16] {'wide'}, dimensions={0}, use_global_device_ids=true | all-gather | bytes 835584 | tf_op jit(solution)/shard_map/all_gather | solution.py:147
  86.3 6.4 %fusion.39 = f32[128,2048]{1,0:T(8,128)S(1)} fusion(bf16[128,3072]{1,0:T(8,128)(2,1)S(1)} %all_gather.3, bf16[3072,2048]{1,0:T(8,128)(2,1)} %param.25), kind=kOutput, calls=%fused_computation.71 | convolution fusion | flops 1610612736 | bytes 14417920 | tf_op jit(solution)/shard_map/dot_general | solution.py:148
  92.7 12.9 %convolution_multiply_fusion = f32[128,3072]{1,0:T(8,128)} fusion(bf16[2048,3072]{1,0:T(8,128)(2,1)} %param.27, f32[128]{0:T(128)S(1)} %fusion.33, bf16[128,3072]{1,0:T(8,128)(2,1)S(1)} %all_gather.3, bf16[3072,2048]{1,0:T(8,128)(2,1)} %param.26, f32[128,2048]{1,0:T(8,128)S(1)} %fusion.39), kind=kOutput, calls=%fused_computation | convolution fusion | flops 3223191552 | bytes 28574208 | tf_op jit(solution)/shard_map/dot_general | solution.py:152
  105.6 56.9 %reduce-scatter.2.cloned.1.call-done = f32[8,3072]{1,0:T(8,128)} async-done(((f32[128,3072]{1,0:T(8,128)}), f32[8,3072]{1,0:T(8,128)}) %reduce-scatter.2.cloned.1.call-update) | async-done | bytes 98320 | tf_op jit(solution)/shard_map/reduce_scatter | solution.py:151
  162.6 1.5 convert_element_type.53
  (33 shorter events, 0.5 us)
Async XLA Ops:
  7.2 14.9 %copy-start = (bf16[8,64,512]{2,1,0:T(8,128)(2,1)S(1)}, bf16[8,64,512]{2,1,0:T(8,128)(2,1)}, u32[]{:S(2)}) copy-start(bf16[8,64,512]{2,1,0:T(8,128)(2,1)} %param.19) | copy-start | bytes 1572868
  7.2 14.0 %copy-start.1 = (bf16[512,512]{1,0:T(8,128)(2,1)S(1)}, bf16[512,512]{1,0:T(8,128)(2,1)}, u32[]{:S(2)}) copy-start(bf16[512,512]{1,0:T(8,128)(2,1)} %param.17) | copy-start | bytes 1572868
  8.3 13.0 %copy-start.2 = (bf16[8,64,512]{2,1,0:T(8,128)(2,1)S(1)}, bf16[8,64,512]{2,1,0:T(8,128)(2,1)}, u32[]{:S(2)}) copy-start(bf16[8,64,512]{2,1,0:T(8,128)(2,1)} %param.18) | copy-start | bytes 1572868
  8.3 13.0 %copy-start.3 = (bf16[8,3072]{1,0:T(8,128)(2,1)S(1)}, bf16[8,3072]{1,0:T(8,128)(2,1)}, u32[]{:S(2)}) copy-start(bf16[8,3072]{1,0:T(8,128)(2,1)} %param.14) | copy-start | bytes 147460
  10.4 16.4 %all-to-all-start = ((bf16[16,2,3072]{2,1,0:T(2,128)(2,1)}), bf16[16,2,3072]{2,1,0:T(2,128)(2,1)S(1)}, u32[]{:S(2)}, u32[]{:S(2)}) async-start(bf16[16,2,3072]{2,1,0:T(2,128)(2,1)} %copy.75), calls=%async_computation | async-start | bytes 393216 | tf_op jit(solution)/shard_map/all_to_all | solution.py:124
  28.2 10.0 %all-to-all-start.2 = ((f32[16,2,24]{2,1,0:T(2,128)}), f32[16,2,24]{2,1,0:T(2,128)S(1)}, u32[]{:S(2)}, u32[]{:S(2)}) async-start(f32[16,2,24]{2,1,0:T(2,128)} %reshape_reshape.14), calls=%async_computation.2 | async-start | bytes 32768 | tf_op jit(solution)/shard_map/all_to_all | solution.py:131
  38.2 10.0 %all-to-all-start.3 = ((f32[16,2,24]{2,1,0:T(2,128)}), f32[16,2,24]{2,1,0:T(2,128)S(1)}, u32[]{:S(2)}, u32[]{:S(2)}) async-start(f32[16,2,24]{2,1,0:T(2,128)} %reshape_reshape.15), calls=%async_computation.3 | async-start | bytes 32768 | tf_op jit(solution)/shard_map/all_to_all | solution.py:134
  42.1 9.6 %copy-start.8 = (f32[128,2]{0,1:T(2,128)S(1)}, f32[128,2]{0,1:T(2,128)}, u32[]{:S(2)}) copy-start(f32[128,2]{0,1:T(2,128)} %param.23) | copy-start | bytes 3076
  42.1 9.6 %copy-start.9 = (s32[128,2]{0,1:T(2,128)S(1)}, s32[128,2]{0,1:T(2,128)}, u32[]{:S(2)}) copy-start(s32[128,2]{0,1:T(2,128)} %param.22) | copy-start | bytes 3076
  42.1 9.7 %copy-start.4 = (f32[8,4,6,128]{3,2,1,0:T(8,128)S(1)}, f32[8,4,6,128]{3,2,1,0:T(8,128)}, u32[]{:S(2)}) copy-start(f32[8,4,6,128]{3,2,1,0:T(8,128)} %fusion.8) | copy-start | bytes 294916
  42.4 21.7 %copy-start.5 = (bf16[8,3072]{1,0:T(8,128)(2,1)S(1)}, bf16[8,3072]{1,0:T(8,128)(2,1)}, u32[]{:S(2)}) copy-start(bf16[8,3072]{1,0:T(8,128)(2,1)} %param.15) | copy-start | bytes 147460
  43.4 21.6 %copy-start.7 = (f32[3072]{0:T(1024)S(1)}, f32[3072]{0:T(1024)}, u32[]{:S(2)}) copy-start(f32[3072]{0:T(1024)} %param.24) | copy-start | bytes 36868
  48.1 15.7 %all-to-all-start.1 = ((f32[16,2,3072]{2,1,0:T(2,128)}), f32[16,2,3072]{2,1,0:T(2,128)S(1)}, u32[]{:S(2)}, u32[]{:S(2)}) async-start(f32[16,2,3072]{2,1,0:T(2,128)} %reshape_reshape.13), calls=%async_computation.1 | async-start | bytes 786432 | tf_op jit(solution)/shard_map/all_to_all | solution.py:128
  51.7 110.9 %reduce-scatter.2.cloned.1.call-start = ((), (), s32[]{:S(2)}) async-start(), calls=%async_computation.5 | async-start | bytes 1671168 | tf_op jit(solution)/shard_map/reduce_scatter | solution.py:151
  64.9 27.8 %copy-start.6 = (bf16[8,3072]{1,0:T(8,128)(2,1)}, bf16[8,3072]{1,0:T(8,128)(2,1)S(1)}, u32[]{:S(2)}) copy-start(bf16[8,3072]{1,0:T(8,128)(2,1)S(1)} %get-tuple-element.9) | copy-start | bytes 147460
Sparse Core Ops, SparseCore 0:
  105.8 56.7 reduce-scatter.1
where the time goes:
time: 172 us; the launch traced here: 171 us
  waiting for transfers between devices  81.4 us (47%)
  matrix products  23.6 us (14%)
  blocking collectives  21.3 us (12%)
  starting transfers between devices  18 us (10%)
  between operations  14.3 us (8%)
  local copies, waits for them, and re-layouts  7.13 us (4%)
  other arithmetic  5.26 us (3%)
    reduce_scatter x1, waiting for transfers between devices, local(): lax.psum_scatter(share[:, None] * jnp.dot(hidden_all, down_weight, prefer...  56.9 us
    all_gather x1, blocking collectives, local(): piece = lax.all_gather(normed, 'wide', axis=0, tiled=True)  21.3 us
    dot_general x1, matrix products, local(): jnp.dot(hidden_all, down_weight, preferred_element_type=jnp.float32)  12.9 us
    all_to_all x1, waiting for transfers between devices, local(): lax.all_to_all(part_out.reshape(devices, slot_count, D), 'wide', split_ax...  10.8 us
    all_to_all x1, starting transfers between devices, local(): lax.all_to_all(outgoing, 'wide', split_axis=0, concat_axis=0, tiled=True)  7.41 us
    dot_general x1, matrix products, local(): gate_part = jnp.dot(piece, gate_weight, preferred_element_type=jnp.float32)  6.36 us
    all_to_all x1, waiting for transfers between devices, local(): lax.all_to_all(part_max.reshape(devices, slot_count, HQ), 'wide', split_a...  5.11 us
    all_to_all x1, waiting for transfers between devices, local(): lax.all_to_all(part_sum.reshape(devices, slot_count, HQ), 'wide', split_a...  4.76 us
  transfers between devices with their start and end apart: 5, of which 5 were waited for; matrix products, arithmetic and copies ran while one was open for 5% of the time, Pallas kernels for 0%

commit v1 on v0

v1 whole, which is shorter than its diff:
```python
import math

import jax
import jax.numpy as jnp
from jax import lax
from jax.sharding import PartitionSpec as P

HQ = 24
HK = 4
DH = 128
EXPERTS = 4
PREFIXES = 8
CAPP = 2
STAT = 128

masked_score = -1e30


def split_parts(x, parts):
    pieces = []
    for _ in range(parts):
        piece = lax.reduce_precision(x, 8, 7)
        pieces.append(piece.astype(jnp.bfloat16))
        x = x - piece
    return pieces


def attend(query_rows, key_rows, value_rows):
    rows, width = query_rows.shape
    query_heads = query_rows.reshape(rows, HK, HQ // HK, DH)
    key_heads = key_rows.reshape(key_rows.shape[0], HK, DH)
    value_heads = value_rows.reshape(value_rows.shape[0], HK, DH)
    scores = jnp.einsum(
        "nkgd,pkd->nkgp", query_heads, key_heads, preferred_element_type=jnp.float32
    ) * (1.0 / math.sqrt(DH))
    block_max = jnp.max(scores, axis=-1)
    weights = jnp.exp(scores - block_max[..., None]).astype(jnp.bfloat16)
    block_sum = jnp.sum(weights.astype(jnp.float32), axis=-1)
    block_out = jnp.einsum(
        "nkgp,pkd->nkgd", weights, value_heads, preferred_element_type=jnp.float32
    )
    return block_out.reshape(rows, width), block_max.reshape(rows, HQ), block_sum.reshape(rows, HQ)


def attend_suffix(query_rows, key_rows, value_rows, lengths):
    rows = query_rows.shape[0]
    slots_max = key_rows.shape[1]
    query_heads = query_rows.reshape(rows, HK, HQ // HK, DH)
    key_heads = key_rows.reshape(rows, slots_max, HK, DH)
    value_heads = value_rows.reshape(rows, slots_max, HK, DH)
    scores = jnp.einsum(
        "nkgd,nskd->nkgs", query_heads, key_heads, preferred_element_type=jnp.float32
    ) * (1.0 / math.sqrt(DH))
    usable = jnp.arange(slots_max)[None, :] < lengths[:, None]
    scores = jnp.where(usable[:, None, None, :], scores, masked_score)
    block_max = jnp.max(scores, axis=-1)
    weights = jnp.exp(scores - block_max[..., None]).astype(jnp.bfloat16)
    block_sum = jnp.sum(weights.astype(jnp.float32), axis=-1)
    block_out = jnp.einsum(
        "nkgs,nskd->nkgd", weights, value_heads, preferred_element_type=jnp.float32
    )
    return block_out.reshape(rows, HQ, DH), block_max.reshape(rows, HQ), block_sum.reshape(rows, HQ)


def slot_table(owned_keys, device_key, capacity):
    entries = owned_keys.shape[0]
    alike_key = owned_keys[:, None] == owned_keys[None, :]
    position = jnp.arange(entries)
    earlier = position[None, :] < position[:, None]
    slot_rank = jnp.sum(alike_key & earlier, axis=1)
    matches = device_key[:, None, None] == owned_keys[None, None, :]
    placed = slot_rank[None, None, :] == jnp.arange(capacity)[None, :, None]
    return matches & placed


def merge_parts(part_out, part_max, part_sum, selection, suffix_out, suffix_max, suffix_sum):
    sources, slot_count = (part_max.shape[0], part_max.shape[1])
    rows = suffix_out.shape[0]
    masked = jnp.where(selection[..., None], part_max[:, :, None, :], masked_score)
    overall = jnp.maximum(jnp.max(masked, axis=(0, 1)), suffix_max)
    factor = jnp.where(selection[..., None], jnp.exp(masked - overall[None, None]), 0.0)
    out_heads = part_out.reshape(sources, slot_count, HQ, DH).astype(jnp.float32)
    suffix_factor = jnp.exp(suffix_max - overall)
    numerator = (
        jnp.einsum("scnh,schd->nhd", factor, out_heads, precision=lax.Precision.HIGHEST)
        + suffix_factor[..., None] * suffix_out
    )
    denominator = (
        jnp.einsum("scnh,sch->nh", factor, part_sum, precision=lax.Precision.HIGHEST)
        + suffix_factor * suffix_sum
    )
    return (numerator / denominator[..., None]).reshape(rows, HQ * DH).astype(jnp.bfloat16)


def local(
    queries,
    hidden_in,
    prefix_keys,
    prefix_values,
    suffix_keys,
    suffix_values,
    suffix_length,
    prefix_of,
    expert_index,
    gate_logits,
    norm_gain,
    gate_weight,
    up_weight,
    down_weight,
):
    devices = lax.axis_size("wide")
    rank_here = lax.axis_index("wide")
    rows, width = queries.shape
    half = devices // 2
    start_row = rank_here * rows
    siblings = [(i, i ^ 1) for i in range(devices)]
    alike = [[2 * i + c for i in range(half)] for c in range(2)]

    own_prefix = lax.dynamic_slice_in_dim(prefix_of[:, 0], start_row, rows, 0)
    selection = slot_table(own_prefix, jnp.arange(devices) // (devices // PREFIXES), CAPP)
    outgoing = jnp.einsum(
        "sci,id->scd", selection.astype(jnp.bfloat16), queries, preferred_element_type=jnp.float32
    ).astype(jnp.bfloat16)
    received = lax.all_to_all(outgoing, "wide", split_axis=0, concat_axis=0, tiled=True)
    suffix_out, suffix_max, suffix_sum = attend_suffix(
        queries, suffix_keys, suffix_values, suffix_length
    )
    part_out, part_max, part_sum = attend(
        received.reshape(devices * CAPP, width), prefix_keys, prefix_values
    )
    pieces = split_parts(part_max, 3) + split_parts(part_sum, 2)
    pad = jnp.zeros((devices * CAPP, STAT - 5 * HQ), jnp.bfloat16)
    packed = jnp.concatenate([part_out.astype(jnp.bfloat16)] + pieces + [pad], axis=1)
    back = lax.all_to_all(
        packed.reshape(devices, CAPP, width + STAT), "wide", split_axis=0, concat_axis=0, tiled=True
    )
    stats = back[:, :, width : width + 5 * HQ].astype(jnp.float32).reshape(devices, CAPP, 5, HQ)
    back_max = stats[:, :, 0] + stats[:, :, 1] + stats[:, :, 2]
    back_sum = stats[:, :, 3] + stats[:, :, 4]
    attended = merge_parts(
        back[:, :, :width], back_max, back_sum, selection, suffix_out, suffix_max, suffix_sum
    )
    stream = hidden_in.astype(jnp.float32) + attended.astype(jnp.float32)
    normed = (
        stream * lax.rsqrt(jnp.mean(stream * stream, axis=-1, keepdims=True) + 1e-05) * norm_gain
    ).astype(jnp.bfloat16)

    spread = jnp.broadcast_to(normed[None], (half, rows, width))
    near = lax.all_to_all(
        spread, "wide", split_axis=0, concat_axis=0, tiled=True, axis_index_groups=alike
    ).reshape(half * rows, width)
    far = lax.ppermute(near, "wide", siblings)
    piece = jnp.concatenate([near, far], axis=0)
    gate_part = jnp.dot(piece, gate_weight, preferred_element_type=jnp.float32)
    up_part = jnp.dot(piece, up_weight, preferred_element_type=jnp.float32)
    hidden_all = (jax.nn.silu(gate_part) * up_part).astype(jnp.bfloat16)
    partial = jnp.dot(hidden_all, down_weight, preferred_element_type=jnp.float32)
    swapped = lax.ppermute(partial[half * rows :], "wide", siblings)
    summed = (partial[: half * rows] + swapped).astype(jnp.bfloat16)
    parts = lax.all_to_all(
        summed.reshape(half, rows, width),
        "wide",
        split_axis=0,
        concat_axis=0,
        tiled=True,
        axis_index_groups=alike,
    )

    own_experts = lax.dynamic_slice_in_dim(expert_index, start_row, rows, 0)
    gates = jax.nn.softmax(lax.dynamic_slice_in_dim(gate_logits, start_row, rows, 0), axis=-1)
    expert_of = (2 * jnp.arange(half)) // (devices // EXPERTS)
    share = jnp.sum(
        gates[None] * (own_experts[None] == expert_of[:, None, None]).astype(jnp.float32), axis=2
    )
    mixture = jnp.sum(share[:, :, None] * parts.astype(jnp.float32), axis=0)
    return (attended, mixture.astype(jnp.bfloat16))


def solution(mesh):
    placed = (
        P(("groups", "wide"), None),
        P(("groups", "wide"), None),
        P(("groups", "wide"), None),
        P(("groups", "wide"), None),
        P(("groups", "wide"), None, None),
        P(("groups", "wide"), None, None),
        P(("groups", "wide")),
        P("groups", None),
        P("groups", None),
        P("groups", None),
        P(),
        P(None, "wide"),
        P(None, "wide"),
        P("wide", None),
    )
    return jax.shard_map(
        local,
        mesh=mesh,
        in_specs=placed,
        out_specs=(P(("groups", "wide"), None), P(("groups", "wide"), None)),
        check_vma=False,
    )
```

time: 172 us -> 93.8 us (0.55)
  waiting for transfers between devices: 81.4 us -> 29.8 us
  between operations: 14.3 us -> 1.12 us
  blocking collectives: 21.3 us -> 14.7 us
  starting transfers between devices: 18 us -> 14.7 us
  matrix products: 23.6 us -> 21.7 us
    reduce_scatter x1 -> x0, waiting for transfers between devices: 56.9 us -> none  [local(): lax.psum_scatter(share[:, None] * jnp.dot(hidden_all, down_weight, prefer...]
    all_gather x1 -> x0, blocking collectives: 21.3 us -> none  [local(): piece = lax.all_gather(normed, 'wide', axis=0, tiled=True)]
    all_to_all x0 -> x1, blocking collectives: none -> 14.7 us  [local(): lax.all_to_all(spread, 'wide', split_axis=0, concat_axis=0, tiled=True, a...]
    ppermute x0 -> x2, waiting for transfers between devices: none -> 4 us  [the longest x1 2.15 us: local(): swapped = lax.ppermute(partial[half * rows:], 'wide', siblings)]
    all_to_all x3 -> x2, starting transfers between devices: 10.5 us -> 7.11 us  [the longest x1 3.65 us: local(): lax.all_to_all(packed.reshape(devices, CAPP, width + STAT), 'wide', split...]
    another operation x4 -> x1, local copies, waits for them, and re-layouts: 2.56 us -> 0.17 us  [attend(): query_heads = query_rows.reshape(rows, HK, HQ // HK, DH)]
    all_to_all x1, waiting for transfers between devices: 3.73 us -> 5.5 us  [local(): lax.all_to_all(outgoing, 'wide', split_axis=0, concat_axis=0, tiled=True)]
    all_to_all x3 -> x2, waiting for transfers between devices: 20.7 us -> 20.3 us  [the longest x1 11.7 us: local(): lax.all_to_all(summed.reshape(half, rows, width), 'wide', split_axis=0, c...]
where the time goes in v1:
time: 93.8 us; the launch traced here: 93.2 us
  waiting for transfers between devices  29.8 us (32%)
  matrix products  21.7 us (23%)
  starting transfers between devices  14.7 us (16%)
  blocking collectives  14.7 us (16%)
  local copies, waits for them, and re-layouts  7.54 us (8%)
  other arithmetic  3.65 us (4%)
  between operations  1.12 us (1%)
    all_to_all x1, blocking collectives, local(): lax.all_to_all(spread, 'wide', split_axis=0, concat_axis=0, tiled=True, a...  14.7 us
    dot_general x1, matrix products, local(): jnp.dot(hidden_all, down_weight, preferred_element_type=jnp.float32)  11.9 us
    all_to_all x1, waiting for transfers between devices, local(): lax.all_to_all(summed.reshape(half, rows, width), 'wide', split_axis=0, c...  11.7 us
    all_to_all x1, waiting for transfers between devices, local(): lax.all_to_all(packed.reshape(devices, CAPP, width + STAT), 'wide', split...  8.56 us
    all_to_all x1, starting transfers between devices, local(): lax.all_to_all(outgoing, 'wide', split_axis=0, concat_axis=0, tiled=True)  7.41 us
    dot_general x1, matrix products, local(): up_part = jnp.dot(piece, up_weight, preferred_element_type=jnp.float32)  6.51 us
    all_to_all x1, waiting for transfers between devices, local(): lax.all_to_all(outgoing, 'wide', split_axis=0, concat_axis=0, tiled=True)  5.5 us
    all_to_all x1, starting transfers between devices, local(): lax.all_to_all(packed.reshape(devices, CAPP, width + STAT), 'wide', split...  3.65 us
  transfers between devices with their start and end apart: 5, of which 5 were waited for; matrix products, arithmetic and copies ran while one was open for 5% of the time, Pallas kernels for 0%

profile of v1, /device:TPU:0, one launch (start us, length us, event | category | flops | bytes accessed | tf_op | source)
XLA Modules:
  0.0 93.2 jit_solution(9096015284324940565)
XLA Ops:
  0.7 0.8 fusion.44
  1.5 0.2 convert_reduce_fusion.2
  1.8 1.1 %convolution_convert_fusion = bf16[16,2,3072]{2,0,1:T(8,128)(2,1)S(1)} fusion(bf16[8,3072]{1,0:T(8,128)(2,1)} %param.14, pred[2,8]{1,0:T(4,128)(4,1)S(1)} %iota_compare_fusion.2, pred[16,8]{0,1:T(8,128)(4,1)S(1)} %broadcast_compare_fusion), kind=kOutput, calls=%fused_computation | convolution fusion | flops 1671424 | bytes 245904 | tf_op jit(solution)/shard_map/sci,id->scd/dot_general | solution.py:121
  2.9 0.9 copy.126
  3.8 7.4 %all-to-all-start = ((bf16[16,2,3072]{2,1,0:T(2,128)(2,1)}), bf16[16,2,3072]{2,1,0:T(2,128)(2,1)S(1)}, u32[]{:S(2)}, u32[]{:S(2)}) async-start(bf16[16,2,3072]{2,1,0:T(2,128)(2,1)} %copy.126), calls=%async_computation | async-start | bytes 393216 | tf_op jit(solution)/shard_map/all_to_all | solution.py:124
  11.2 1.2 %reshape.217 = bf16[512,4,128]{2,1,0:T(4,128)(2,1)S(1)} reshape(bf16[512,512]{1,0:T(8,128)(2,1)} %param.16) | data formatting | bytes 1048576 | tf_op jit(solution)/shard_map/reshape | solution.py:31
  12.4 0.1 reshape.218
  12.6 0.5 fusion.52
  13.1 0.7 reshape.226
  13.8 0.2 convert_reduce_fusion.1
  14.0 0.7 reshape.229
  14.7 5.5 %all-to-all-done = bf16[16,2,3072]{2,1,0:T(2,128)(2,1)S(1)} async-done(((bf16[16,2,3072]{2,1,0:T(2,128)(2,1)}), bf16[16,2,3072]{2,1,0:T(2,128)(2,1)S(1)}, u32[]{:S(2)}, u32[]{:S(2)}) %all-to-all-start) | async-done | bytes 196640 | tf_op jit(solution)/shard_map/all_to_all | solution.py:124
  20.2 0.2 reshape_reshape.3
  20.4 0.5 bitcast_reduce_fusion
  20.8 0.1 copy.131
  21.0 0.5 convert_reduce_fusion
  21.5 0.1 copy.134
  21.6 0.1 reshape.220
  21.7 0.4 fusion.2
  22.2 0.1 copy.130
  22.3 0.1 convert_element_type.84
  22.4 0.1 reshape.219
  22.6 1.2 %concatenate.7 = bf16[16,2,3200]{2,1,0:T(2,128)(2,1)} concatenate(bf16[16,2,3072]{2,1,0:T(2,128)(2,1)S(1)} %convert_element_type.84, bf16[16,2,24]{2,1,0:T(2,128)(2,1)S(1)} %copy.135, bf16[16,2,24]{2,1,0:T(2,128)(2,1)S(1)} %copy.136, bf16[16,2,24]{2,1,0:T(2,128)(2,1)S(1)} %copy.137, bf16[16,2,24]{2,1,0:T(2,128)(2,1)S(1)} %get-tuple-element.7, ...), dimensions={2} | concatenate | bytes 409600 | tf_op jit(solution)/shard_map/concatenate | solution.py:133
  23.8 3.7 %all-to-all-start.1 = ((bf16[16,2,3200]{2,1,0:T(2,128)(2,1)}), bf16[16,2,3200]{2,1,0:T(2,128)(2,1)S(1)}, u32[]{:S(2)}, u32[]{:S(2)}) async-start(bf16[16,2,3200]{2,1,0:T(2,128)(2,1)} %concatenate.7), calls=%async_computation.1 | async-start | bytes 409600 | tf_op jit(solution)/shard_map/all_to_all | solution.py:134
  27.5 0.3 fusion.10
  28.0 8.6 %all-to-all-done.1 = bf16[16,2,3200]{2,1,0:T(2,128)(2,1)S(1)} async-done(((bf16[16,2,3200]{2,1,0:T(2,128)(2,1)}), bf16[16,2,3200]{2,1,0:T(2,128)(2,1)S(1)}, u32[]{:S(2)}, u32[]{:S(2)}) %all-to-all-start.1) | async-done | bytes 204832 | tf_op jit(solution)/shard_map/all_to_all | solution.py:134
  36.5 0.1 reshape.233
  36.7 0.1 copy.140
  36.8 0.1 select_reduce_fusion
  37.0 0.1 copy.167
  37.1 0.2 fusion.27
  37.5 0.1 slice.36
  37.7 0.1 reshape.240
  37.8 0.1 bitcast_multiply_fusion
  37.9 0.5 multiply_reduce_fusion.1
  38.5 0.1 multiply_convert_fusion.2
  38.6 14.7 %all_to_all.20 = bf16[8,8,3072]{2,1,0:T(8,128)(2,1)S(1)} all-to-all(bf16[8,8,3072]{2,1,0:T(8,128)(2,1)S(1)} %broadcast_in_dim.56), channel_id=1, replica_groups={{0,2,4,6,8,10,12,14},{1,3,5,7,9,11,13,15},{16,18,20,22,24,26,28,30},{17..., dimensions={0} | all-to-all | bytes 786432 | tf_op jit(solution)/shard_map/all_to_all | solution.py:149
  53.3 1.9 %collective-permute-done = bf16[64,3072]{1,0:T(8,128)(2,1)} collective-permute-done((bf16[64,3072]{1,0:T(8,128)(2,1)S(1)}, bf16[64,3072]{1,0:T(8,128)(2,1)}, u32[]{:S(2)}, u32[]{:S(2)}) %collective-permute-start) | collective-permute-done | bytes 393248 | tf_op jit(solution)/shard_map/ppermute | solution.py:152
  55.2 6.5 %fusion.18 = f32[128,2048]{1,0:T(8,128)S(1)} fusion(bf16[3072,2048]{1,0:T(8,128)(2,1)} %param.26, bf16[64,3072]{1,0:T(8,128)(2,1)} %collective-permute-done, bf16[64,3072]{1,0:T(8,128)(2,1)S(1)} %bitcast.76), kind=kOutput, calls=%fused_computation.30 | convolution fusion | flops 1612185600 | bytes 14417920 | tf_op jit(solution)/shard_map/dot_general | solution.py:155
  61.7 11.9 %fusion.9 = f32[128,3072]{1,0:T(8,128)S(1)} fusion(bf16[2048,3072]{1,0:T(8,128)(2,1)} %param.27, f32[128,2048]{1,0:T(8,128)S(1)} %fusion.18, bf16[3072,2048]{1,0:T(8,128)(2,1)} %param.25, bf16[64,3072]{1,0:T(8,128)(2,1)} %collective-permute-done, bf16[64,3072]{1,0:T(8,128)(2,1)S(1)} %bitcast.77), kind=kOutput, calls=%fused_computation.21 | convolution fusion | flops 3224371200 | bytes 28573696 | tf_op jit(solution)/shard_map/dot_general | solution.py:157
  73.6 0.2 collective-permute-start.1
  73.8 2.1 %collective-permute-done.1 = f32[64,3072]{1,0:T(8,128)S(1)} collective-permute-done((f32[64,3072]{1,0:T(8,128)S(1)}, f32[64,3072]{1,0:T(8,128)S(1)}, u32[]{:S(2)}, u32[]{:S(2)}) %collective-permute-start.1) | collective-permute-done | bytes 786464 | tf_op jit(solution)/shard_map/ppermute | solution.py:158
  76.0 0.8 fusion.20
  76.8 3.5 %all-to-all-start.3 = ((bf16[8,8,3072]{2,1,0:T(8,128)(2,1)}), bf16[8,8,3072]{2,1,0:T(8,128)(2,1)S(1)}, u32[]{:S(2)}, u32[]{:S(2)}) async-start(bf16[8,8,3072]{2,1,0:T(8,128)(2,1)} %fusion.20), calls=%async_computation.3 | async-start | bytes 786432 | tf_op jit(solution)/shard_map/all_to_all | solution.py:160
  80.3 0.1 fusion.45
  80.5 0.1 fusion.43
  80.7 11.7 %all-to-all-done.3 = bf16[8,8,3072]{2,1,0:T(8,128)(2,1)S(1)} async-done(((bf16[8,8,3072]{2,1,0:T(8,128)(2,1)}), bf16[8,8,3072]{2,1,0:T(8,128)(2,1)S(1)}, u32[]{:S(2)}, u32[]{:S(2)}) %all-to-all-start.3) | async-done | bytes 393248 | tf_op jit(solution)/shard_map/all_to_all | solution.py:160
  92.4 0.8 multiply_reduce_fusion
  (66 shorter events, 1.2 us)
Async XLA Ops:
  0.6 26.8 %copy-start = (bf16[8,64,512]{2,1,0:T(8,128)(2,1)S(1)}, bf16[8,64,512]{2,1,0:T(8,128)(2,1)}, u32[]{:S(2)}) copy-start(bf16[8,64,512]{2,1,0:T(8,128)(2,1)} %param.19) | copy-start | bytes 1572868
  0.6 11.8 %copy-start.1 = (bf16[512,512]{1,0:T(8,128)(2,1)S(1)}, bf16[512,512]{1,0:T(8,128)(2,1)}, u32[]{:S(2)}) copy-start(bf16[512,512]{1,0:T(8,128)(2,1)} %param.17) | copy-start | bytes 1572868
  0.7 11.9 %copy-start.17 = (s32[8]{0:T(128)S(1)}, s32[8]{0:T(128)}, u32[]{:S(2)}) copy-start(s32[8]{0:T(128)} %param.20) | copy-start | bytes 100
  0.7 12.0 %copy-start.2 = (bf16[8,64,512]{2,1,0:T(8,128)(2,1)S(1)}, bf16[8,64,512]{2,1,0:T(8,128)(2,1)}, u32[]{:S(2)}) copy-start(bf16[8,64,512]{2,1,0:T(8,128)(2,1)} %param.18) | copy-start | bytes 1572868
  0.7 11.9 %copy-start.3 = (bf16[8,3072]{1,0:T(8,128)(2,1)S(1)}, bf16[8,3072]{1,0:T(8,128)(2,1)}, u32[]{:S(2)}) copy-start(bf16[8,3072]{1,0:T(8,128)(2,1)} %param.14) | copy-start | bytes 147460
  1.8 11.3 %copy-start.11 = (pred[16,8]{0,1:T(8,128)(4,1)}, pred[16,8]{0,1:T(8,128)(4,1)S(1)}, u32[]{:S(2)}) copy-start(pred[16,8]{0,1:T(8,128)(4,1)S(1)} %broadcast_compare_fusion) | copy-start | bytes 388
  1.8 11.3 %copy-start.14 = (pred[2,8]{1,0:T(4,128)(4,1)}, pred[2,8]{1,0:T(4,128)(4,1)S(1)}, u32[]{:S(2)}) copy-start(pred[2,8]{1,0:T(4,128)(4,1)S(1)} %iota_compare_fusion.2) | copy-start | bytes 52
  3.8 16.4 %all-to-all-start = ((bf16[16,2,3072]{2,1,0:T(2,128)(2,1)}), bf16[16,2,3072]{2,1,0:T(2,128)(2,1)S(1)}, u32[]{:S(2)}, u32[]{:S(2)}) async-start(bf16[16,2,3072]{2,1,0:T(2,128)(2,1)} %copy.126), calls=%async_computation | async-start | bytes 393216 | tf_op jit(solution)/shard_map/all_to_all | solution.py:124
  13.1 1.6 %copy-start.4 = (f32[8,4,6]{2,1,0:T(4,128)}, f32[8,4,6]{2,1,0:T(4,128)S(1)}, u32[]{:S(2)}) copy-start(f32[8,4,6]{2,1,0:T(4,128)S(1)} %get-tuple-element.11) | copy-start | bytes 2308
  21.7 5.7 %copy-start.5 = (f32[8,4,6]{2,1,0:T(4,128)S(1)}, f32[8,4,6]{2,1,0:T(4,128)}, u32[]{:S(2)}) copy-start(f32[8,4,6]{2,1,0:T(4,128)} %copy-done.4) | copy-start | bytes 2308
  22.2 5.7 %copy-start.12 = (pred[16,8]{0,1:T(8,128)(4,1)S(1)}, pred[16,8]{0,1:T(8,128)(4,1)}, u32[]{:S(2)}) copy-start(pred[16,8]{0,1:T(8,128)(4,1)} %copy-done.11) | copy-start | bytes 388
  22.2 5.7 %copy-start.15 = (pred[2,8]{1,0:T(4,128)(4,1)S(1)}, pred[2,8]{1,0:T(4,128)(4,1)}, u32[]{:S(2)}) copy-start(pred[2,8]{1,0:T(4,128)(4,1)} %copy-done.14) | copy-start | bytes 52
  22.3 14.6 %copy-start.8 = (f32[8,24]{1,0:T(8,128)S(1)}, f32[8,24]{1,0:T(8,128)}, u32[]{:S(2)}) copy-start(f32[8,24]{1,0:T(8,128)} %reshape.226) | copy-start | bytes 2308
  22.3 15.1 %copy-start.9 = (f32[8,24]{1,0:T(8,128)S(1)}, f32[8,24]{1,0:T(8,128)}, u32[]{:S(2)}) copy-start(f32[8,24]{1,0:T(8,128)} %reshape.229) | copy-start | bytes 2308
  23.8 14.1 %copy-start.6 = (bf16[8,3072]{1,0:T(8,128)(2,1)S(1)}, bf16[8,3072]{1,0:T(8,128)(2,1)}, u32[]{:S(2)}) copy-start(bf16[8,3072]{1,0:T(8,128)(2,1)} %param.15) | copy-start | bytes 147460
  23.8 12.7 %all-to-all-start.1 = ((bf16[16,2,3200]{2,1,0:T(2,128)(2,1)}), bf16[16,2,3200]{2,1,0:T(2,128)(2,1)S(1)}, u32[]{:S(2)}, u32[]{:S(2)}) async-start(bf16[16,2,3200]{2,1,0:T(2,128)(2,1)} %concatenate.7), calls=%async_computation.1 | async-start | bytes 409600 | tf_op jit(solution)/shard_map/all_to_all | solution.py:134
  27.8 10.7 %copy-start.10 = (f32[3072]{0:T(1024)S(1)}, f32[3072]{0:T(1024)}, u32[]{:S(2)}) copy-start(f32[3072]{0:T(1024)} %param.24) | copy-start | bytes 36868
  38.5 16.7 %copy-start.7 = (bf16[8,3072]{1,0:T(8,128)(2,1)}, bf16[8,3072]{1,0:T(8,128)(2,1)S(1)}, u32[]{:S(2)}) copy-start(bf16[8,3072]{1,0:T(8,128)(2,1)S(1)} %get-tuple-element.16) | copy-start | bytes 147460
  53.3 1.9 %collective-permute-start = (bf16[64,3072]{1,0:T(8,128)(2,1)S(1)}, bf16[64,3072]{1,0:T(8,128)(2,1)}, u32[]{:S(2)}, u32[]{:S(2)}) collective-permute-start(bf16[64,3072]{1,0:T(8,128)(2,1)S(1)} %bitcast.75), channel_id=1, source_target_pairs={{0,1},{1,0},{2,3},{3,2},{4,5},{5,4},{6,7},{7,6},{8,9},{9,8},{10,11... | collective-permute-start | bytes 1179656 | tf_op jit(solution)/shard_map/ppermute | solution.py:152
  73.6 6.6 %copy-start.13 = (f32[128,2]{0,1:T(2,128)S(1)}, f32[128,2]{0,1:T(2,128)}, u32[]{:S(2)}) copy-start(f32[128,2]{0,1:T(2,128)} %param.23) | copy-start | bytes 3076
  73.6 6.7 %copy-start.16 = (s32[128,2]{0,1:T(2,128)S(1)}, s32[128,2]{0,1:T(2,128)}, u32[]{:S(2)}) copy-start(s32[128,2]{0,1:T(2,128)} %param.22) | copy-start | bytes 3076
  73.6 2.4 %collective-permute-start.1 = (f32[64,3072]{1,0:T(8,128)S(1)}, f32[64,3072]{1,0:T(8,128)S(1)}, u32[]{:S(2)}, u32[]{:S(2)}) collective-permute-start(f32[64,3072]{1,0:T(8,128)S(1)} %slice.44), channel_id=1, source_target_pairs={{0,1},{1,0},{2,3},{3,2},{4,5},{5,4},{6,7},{7,6},{8,9},{9,8},{10,11... | collective-permute-start | bytes 2359304 | tf_op jit(solution)/shard_map/ppermute | solution.py:158
  76.8 15.6 %all-to-all-start.3 = ((bf16[8,8,3072]{2,1,0:T(8,128)(2,1)}), bf16[8,8,3072]{2,1,0:T(8,128)(2,1)S(1)}, u32[]{:S(2)}, u32[]{:S(2)}) async-start(bf16[8,8,3072]{2,1,0:T(8,128)(2,1)} %fusion.20), calls=%async_computation.3 | async-start | bytes 786432 | tf_op jit(solution)/shard_map/all_to_all | solution.py:160

commit v2 on v0

v2 whole, which is shorter than its diff:
```python
import math

import jax
import jax.numpy as jnp
from jax import lax
from jax.experimental import pallas as pl
from jax.experimental.pallas import tpu as pltpu
from jax.sharding import PartitionSpec as P

HQ = 24
HK = 4
DH = 128
EXPERTS = 4
PREFIXES = 8
CAPP = 2
CAPE = 6

GROUP = HQ // HK
PIECE = GROUP * DH
STAT = 128
SLOT = 8
BLOCKS = CAPE * HK // SLOT
PER = CAPE // (SLOT - CAPE)

masked_score = -1e30
F32 = jnp.float32
BF16 = jnp.bfloat16
VMEM = pl.BlockSpec(memory_space=pltpu.VMEM)
SMEM = pl.BlockSpec(memory_space=pltpu.SMEM)
HBM = pl.BlockSpec(memory_space=pltpu.HBM)


def iotas(shape):
    return lax.broadcasted_iota(jnp.int32, shape, 0), lax.broadcasted_iota(jnp.int32, shape, 1)


def div(x, m):
    return jnp.right_shift(x, m.bit_length() - 1)


def mod(x, m):
    return jnp.bitwise_and(x, m - 1)


def one_hot(picked):
    return picked.astype(F32).astype(BF16)


def dot(a, b):
    return jnp.dot(a, b, preferred_element_type=F32)


def dot_t(a, b):
    return lax.dot_general(a, b, (((1,), (1,)), ((), ())), preferred_element_type=F32)


def by_row(index, values):
    out = jnp.zeros(index.shape, jnp.asarray(values[0]).dtype)
    for i, value in enumerate(values):
        out = jnp.where(index == i, value, out)
    return out


def prefix_slots(prefix_ref, start, rows):
    named = [prefix_ref[start + r] for r in range(rows)]
    ranks = []
    for r in range(rows):
        rank = jnp.int32(0)
        for q in range(r):
            rank += (named[q] == named[r]).astype(jnp.int32)
        ranks.append(rank)
    return named, ranks


def stack_pieces(x):
    return jnp.concatenate([x[:, k * PIECE : (k + 1) * PIECE] for k in range(HK)], axis=0)


def call(kernel, outs, ins, specs, flops=0, limit=24, scratch=(), moved=0, out_specs=None):
    return pl.pallas_call(
        kernel,
        out_shape=outs,
        in_specs=specs,
        out_specs=out_specs or jax.tree.map(lambda _: VMEM, outs),
        scratch_shapes=scratch,
        compiler_params=pltpu.CompilerParams(vmem_limit_bytes=limit * 1024 * 1024),
        cost_estimate=pl.CostEstimate(
            flops=flops, bytes_accessed=moved or 1 << 20, transcendentals=0
        ),
    )(*ins)


def send_queries(queries, prefix_of, devices):
    rows = queries.shape[0]
    holders = devices // PREFIXES

    def kernel(query_ref, prefix_ref, out_ref):
        start = lax.axis_index("wide") * rows
        named, ranks = prefix_slots(prefix_ref, start, rows)
        row, col = iotas((devices * HK * CAPP, HK * rows))
        device, k, c = div(row, HK * CAPP), mod(div(row, CAPP), HK), mod(row, CAPP)
        r = mod(col, rows)
        picked = (
            (k == div(col, rows)) & (div(device, holders) == by_row(r, named)) & (c == by_row(r, ranks))
        )
        pieces = stack_pieces(query_ref[...].astype(F32)).astype(BF16)
        out_ref[...] = dot(one_hot(picked), pieces).astype(BF16)

    return call(
        kernel,
        jax.ShapeDtypeStruct((devices * HK * CAPP, PIECE), BF16),
        (queries, prefix_of),
        [VMEM, SMEM],
    )


def softmax_block(query, keys, values, mask):
    scores = dot_t(query, keys) * (1.0 / math.sqrt(DH))
    if mask is not None:
        scores = jnp.where(mask, scores, masked_score)
    top = jnp.max(scores, axis=-1, keepdims=True)
    weights = jnp.exp(scores - top).astype(BF16)
    total = jnp.sum(weights.astype(F32), axis=-1, keepdims=True)
    return dot(weights, values), top, total


def heads_of(x):
    return jnp.concatenate([x[:, g * DH : (g + 1) * DH] for g in range(GROUP)], axis=0)


def own_suffix(queries, keys, values, lengths):
    rows = queries.shape[0]
    span = keys.shape[1]
    flat = (rows * span, keys.shape[2])

    def kernel(query_ref, key_ref, value_ref, length_ref, out_ref, stat_ref):
        row, col = iotas((rows, rows * span))
        owner = div(col, span)
        live = (owner == row) & (mod(col, span) < by_row(owner, [length_ref[r] for r in range(rows)]))
        mask = jnp.concatenate([live.astype(F32)] * GROUP, axis=0) > 0.5
        lane = iotas((rows, STAT))[1]
        query = query_ref[...].astype(F32)
        for k in range(HK):
            cols = pl.ds(k * DH, DH)
            own = pl.ds(k * rows, rows)
            out, top, total = softmax_block(
                heads_of(query[:, k * PIECE : (k + 1) * PIECE]).astype(BF16),
                key_ref[:, cols],
                value_ref[:, cols],
                mask,
            )
            stat = jnp.zeros((rows, STAT), F32)
            for g in range(GROUP):
                part = slice(g * rows, (g + 1) * rows)
                out_ref[own, pl.ds(g * DH, DH)] = out[part]
                stat = jnp.where(lane == g, top[part], stat)
                stat = jnp.where(lane == SLOT + g, total[part], stat)
            stat_ref[own, :] = stat

    return call(
        kernel,
        (
            jax.ShapeDtypeStruct((HK * rows, PIECE), F32),
            jax.ShapeDtypeStruct((HK * rows, STAT), F32),
        ),
        (queries, keys.reshape(flat), values.reshape(flat), lengths),
        [VMEM, VMEM, VMEM, SMEM],
        flops=1 << 29,
    )


def prefix_block(received, keys, values, devices):
    total_rows = devices * HK * CAPP
    slots = devices * CAPP

    def kernel(received_ref, key_ref, value_ref, out_ref):
        row, col = iotas((total_rows, total_rows))
        device, slot = mod(div(row, CAPP), devices), mod(row, CAPP)
        to_heads = (device * (HK * CAPP) + div(row, slots) * CAPP + slot) == col
        query = dot(one_hot(to_heads), received_ref[...])
        lane = iotas((slots, STAT))[1]
        field, head = div(lane, SLOT), mod(lane, SLOT)
        packed = []
        for k in range(HK):
            cols = pl.ds(k * DH, DH)
            out, top, total = softmax_block(
                heads_of(query[k * slots : (k + 1) * slots]).astype(BF16),
                key_ref[:, cols],
                value_ref[:, cols],
                None,
            )
            parts = [out[g * slots : (g + 1) * slots] for g in range(GROUP)]
            tops = by_row(head, [top[g * slots : (g + 1) * slots] for g in range(GROUP)])
            sums = by_row(head, [total[g * slots : (g + 1) * slots] for g in range(GROUP)])
            high = tops.astype(BF16).astype(F32)
            middle = (tops - high).astype(BF16).astype(F32)
            low = tops - high - middle
            sum_high = sums.astype(BF16).astype(F32)
            stat = by_row(field, [high, middle, low, sum_high, sums - sum_high])
            packed.append(jnp.concatenate(parts + [stat], axis=1))
        packed = jnp.concatenate(packed, axis=0).astype(BF16)
        device, k = div(row, HK * CAPP), mod(div(row, CAPP), HK)
        to_devices = (k * slots + device * CAPP + slot) == col
        out_ref[...] = dot(one_hot(to_devices), packed).astype(BF16)

    return call(
        kernel,
        jax.ShapeDtypeStruct((total_rows, PIECE + STAT), BF16),
        (received, keys, values),
        [VMEM, VMEM, VMEM],
    )


def routes(expert_index, gate_logits, devices, rows):
    half = devices // 2
    per_expert = half // EXPERTS

    def kernel(expert_ref, logit_ref, pack_ref, main_ref, tail_ref, gate_ref):
        start = lax.axis_index("wide") * rows
        named = [[expert_ref[j, start + r] for r in range(rows)] for j in range(2)]
        logits = [[logit_ref[j, start + r] for r in range(rows)] for j in range(2)]

        row, col = iotas((EXPERTS * SLOT, HK * rows))
        expert, i, k, r = div(row, SLOT), mod(row, SLOT), div(col, rows), mod(col, rows)
        has = (by_row(r, named[0]) == expert) | (by_row(r, named[1]) == expert)
        a, b = iotas((HK * rows, HK * rows))
        earlier = (div(a, rows) == div(b, rows)) & (mod(a, rows) < mod(b, rows))
        rank = dot(one_hot(has), one_hot(earlier)).astype(jnp.int32)
        for n in range(BLOCKS):
            slot = jnp.where(i < CAPE, i, (i - CAPE) * PER + n)
            piece = jnp.where(i < CAPE, n, HK - 1)
            pack_ref[n] = one_hot(has & (rank == slot) & (k == piece))

        row, col = iotas((2 * rows, half * SLOT))
        j, r = div(row, rows), mod(row, rows)
        expert, i = div(div(col, SLOT), per_expert), mod(col, SLOT)
        mine = jnp.where(j == 0, by_row(r, named[0]), by_row(r, named[1]))
        rank = jnp.zeros(row.shape, jnp.int32)
        for q in range(rows):
            same = (mine == named[0][q]) | (mine == named[1][q])
            rank += ((r > q) & same).astype(jnp.int32)
        here = expert == mine
        main_ref[...] = one_hot(here & (i == rank))
        for n in range(BLOCKS):
            spot = jnp.full(row.shape, -1, jnp.int32)
            for m in range(SLOT - CAPE):
                spot = jnp.where(rank == m * PER + n, CAPE + m, spot)
            tail_ref[n] = one_hot(here & (i == spot))

        row, _ = iotas((rows, STAT))
        first, second = by_row(row, logits[0]), by_row(row, logits[1])
        top = jnp.maximum(first, second)
        first, second = jnp.exp(first - top), jnp.exp(second - top)
        gate_ref[0] = first / (first + second)
        gate_ref[1] = second / (first + second)

    return call(
        kernel,
        (
            jax.ShapeDtypeStruct((BLOCKS, EXPERTS * SLOT, HK * rows), BF16),
            jax.ShapeDtypeStruct((2 * rows, half * SLOT), BF16),
            jax.ShapeDtypeStruct((BLOCKS, 2 * rows, half * SLOT), BF16),
            jax.ShapeDtypeStruct((2, rows, STAT), F32),
        ),
        (expert_index.T, gate_logits.T),
        [SMEM, SMEM],
        flops=1 << 29,
    )


def merge(back, suffix_out, suffix_stat, hidden_in, norm_gain, prefix_of, pack, devices):
    rows, width = hidden_in.shape
    holders = devices // PREFIXES
    half = devices // 2
    per_expert = half // EXPERTS

    def kernel(
        back_ref, suffix_ref, stat_ref, hidden_ref, gain_ref, prefix_ref, pack_ref, out_ref, sent_ref
    ):
        start = lax.axis_index("wide") * rows
        named, ranks = prefix_slots(prefix_ref, start, rows)
        firsts = [named[r] * (holders * HK * CAPP) + ranks[r] for r in range(rows)]
        row, col = iotas((HK * rows, back_ref.shape[0]))
        target = by_row(mod(row, rows), firsts) + div(row, rows) * CAPP
        stat = stat_ref[...]
        outs, tops, sums = [suffix_ref[...]], [stat[:, :SLOT]], [stat[:, SLOT : 2 * SLOT]]
        for h in range(holders):
            found = dot(one_hot(target + h * (HK * CAPP) == col), back_ref[...])
            stat = found[:, PIECE:]
            field = [stat[:, n * SLOT : (n + 1) * SLOT] for n in range(5)]
            outs.append(found[:, :PIECE])
            tops.append(field[0] + field[1] + field[2])
            sums.append(field[3] + field[4])
        overall = tops[0]
        for top in tops[1:]:
            overall = jnp.maximum(overall, top)
        factors = [jnp.exp(top - overall) for top in tops]
        scale = 1.0 / sum(f * s for f, s in zip(factors, sums))
        factors = [f * scale for f in factors]
        merged = []
        for g in range(GROUP):
            cols = slice(g * DH, (g + 1) * DH)
            merged.append(sum(o[:, cols] * f[:, g : g + 1] for o, f in zip(outs, factors)))
        attended = jnp.concatenate(merged, axis=1).astype(BF16).astype(F32)
        for k in range(HK):
            out_ref[:, pl.ds(k * PIECE, PIECE)] = attended[k * rows : (k + 1) * rows].astype(BF16)
        stream = stack_pieces(hidden_ref[...].astype(F32)) + attended
        squares = jnp.sum(stream * stream, axis=-1, keepdims=True)
        mean = sum(squares[k * rows : (k + 1) * rows] for k in range(HK)) * (1.0 / width)
        scale = jnp.concatenate([lax.rsqrt(mean + 1e-05)] * HK, axis=0)
        gain = jnp.concatenate(
            [
                jnp.broadcast_to(gain_ref[:, k * PIECE : (k + 1) * PIECE], (rows, PIECE))
                for k in range(HK)
            ],
            axis=0,
        )
        normed = (stream * scale * gain).astype(BF16)
        for n in range(BLOCKS):
            taken = dot(pack_ref[n], normed)
            for i in range(half):
                e = i // per_expert
                sent_ref[pl.ds(i * SLOT, SLOT), pl.ds(n * PIECE, PIECE)] = taken[
                    e * SLOT : (e + 1) * SLOT
                ].astype(BF16)

    return call(
        kernel,
        (
            jax.ShapeDtypeStruct((rows, width), BF16),
            jax.ShapeDtypeStruct((half * SLOT, BLOCKS * PIECE), BF16),
        ),
        (back, suffix_out, suffix_stat, hidden_in, norm_gain.reshape(1, width), prefix_of, pack),
        [VMEM, VMEM, VMEM, VMEM, VMEM, SMEM, VMEM],
    )


def cuts(total, step):
    return [(p, min(step, total - p)) for p in range(0, total, step)]


def experts(near, far, gate_weight, up_weight, down_weight):
    half = near.shape[0]
    units, width = down_weight.shape
    depth = 4
    unit_cuts = cuts(units, 512)
    out_cuts = cuts(width, 512)

    def kernel(
        near_ref, far_ref, gate_hbm, up_hbm, down_hbm, mine_ref, theirs_ref,
        gate_ref, up_ref, down_ref, rows_ref, hidden_ref, sems,
    ):
        copies = []
        for p, step in unit_cuts:
            copies.append((gate_hbm, gate_ref, pl.ds(p, step)))
            copies.append((up_hbm, up_ref, pl.ds(p, step)))
        for p, step in out_cuts:
            copies.append((down_hbm, down_ref, pl.ds(p, step)))

        def copy(n):
            source, target, cols = copies[n]
            return pltpu.make_async_copy(source.at[:, cols], target.at[:, cols], sems.at[n])

        for n in range(min(depth, len(copies))):
            copy(n).start()

        def arrive(n):
            copy(n).wait()
            if n + depth < len(copies):
                copy(n + depth).start()

        row, col = iotas((half, half))
        i, i_from = mod(row, SLOT), mod(col, SLOT)
        same = div(row, SLOT) == div(col, SLOT)
        for side, ref in enumerate((near_ref, far_ref)):
            own = pl.ds(side * half, half)
            tail = jnp.zeros((half, PIECE), F32)
            for n in range(BLOCKS):
                spot = jnp.full(row.shape, -1, jnp.int32)
                for m in range(SLOT - CAPE):
                    spot = jnp.where(i == m * PER + n, CAPE + m, spot)
                tail += dot(one_hot(same & (i_from == spot)), ref[:, n * PIECE : (n + 1) * PIECE])
            rows_ref[own, : BLOCKS * PIECE] = ref[...]
            rows_ref[own, BLOCKS * PIECE :] = tail.astype(BF16)
        for n, (p, step) in enumerate(unit_cuts):
            cols = pl.ds(p, step)
            arrive(2 * n)
            gate = dot(rows_ref[...], gate_ref[:, cols])
            arrive(2 * n + 1)
            up = dot(rows_ref[...], up_ref[:, cols])
            hidden_ref[:, cols] = (gate / (1.0 + jnp.exp(-gate)) * up).astype(BF16)
        for n, (p, step) in enumerate(out_cuts):
            cols = pl.ds(p, step)
            arrive(2 * len(unit_cuts) + n)
            part = dot(hidden_ref[...], down_ref[:, cols])
            mine_ref[:, cols] = part[:half]
            theirs_ref[:, cols] = part[half:]

    part = jax.ShapeDtypeStruct((half, width), F32)
    return call(
        kernel,
        (part, part),
        (near, far, gate_weight, up_weight, down_weight),
        [VMEM, VMEM, HBM, HBM, HBM],
        flops=12 * half * units * width,
        moved=6 * units * width,
        limit=56,
        scratch=[
            pltpu.VMEM(gate_weight.shape, BF16),
            pltpu.VMEM(up_weight.shape, BF16),
            pltpu.VMEM(down_weight.shape, BF16),
            pltpu.VMEM((2 * half, width), BF16),
            pltpu.VMEM((2 * half, units), BF16),
            pltpu.SemaphoreType.DMA((2 * len(unit_cuts) + len(out_cuts),)),
        ],
    )


def add_and_pack(mine, swapped):
    half, width = mine.shape

    def kernel(mine_ref, swapped_ref, out_ref):
        row, col = iotas((half, half))
        same = div(row, SLOT) == div(col, SLOT)
        i, i_from = mod(row, SLOT), mod(col, SLOT)
        keep = mod(iotas((half, PIECE))[0], SLOT) < CAPE
        last = pl.ds(BLOCKS * PIECE, PIECE)
        tail = (mine_ref[:, last] + swapped_ref[:, last]).astype(BF16)
        for n in range(BLOCKS):
            cols = pl.ds(n * PIECE, PIECE)
            moved = dot(one_hot(same & (i >= CAPE) & (i_from == (i - CAPE) * PER + n)), tail)
            out_ref[:, cols] = jnp.where(keep, mine_ref[:, cols] + swapped_ref[:, cols], moved).astype(BF16)

    return call(
        kernel,
        jax.ShapeDtypeStruct((half, BLOCKS * PIECE), BF16),
        (mine, swapped),
        [VMEM, VMEM],
    )


def mix(parts, main, tail, gates):
    rows = main.shape[0] // 2

    def kernel(part_ref, main_ref, tail_ref, gate_ref, out_ref):
        first, second = gate_ref[0][:, :1], gate_ref[1][:, :1]
        last = jnp.zeros((2 * rows, PIECE), F32)
        for n in range(BLOCKS):
            cols = pl.ds(n * PIECE, PIECE)
            found = dot(main_ref[...], part_ref[:, cols])
            out_ref[:, cols] = (found[:rows] * first + found[rows:] * second).astype(BF16)
            last += dot(tail_ref[n], part_ref[:, cols])
        cols = pl.ds(BLOCKS * PIECE, PIECE)
        out_ref[:, cols] = (last[:rows] * first + last[rows:] * second).astype(BF16)

    return call(
        kernel,
        jax.ShapeDtypeStruct((rows, HK * PIECE), BF16),
        (parts, main, tail, gates),
        [VMEM, VMEM, VMEM, VMEM],
    )


def exchange(x, groups=None):
    return lax.all_to_all(x, "wide", 0, 0, tiled=True, axis_index_groups=groups)


def local(
    queries,
    hidden_in,
    prefix_keys,
    prefix_values,
    suffix_keys,
    suffix_values,
    suffix_length,
    prefix_of,
    expert_index,
    gate_logits,
    norm_gain,
    gate_weight,
    up_weight,
    down_weight,
):
    devices = lax.axis_size("wide")
    rows = queries.shape[0]
    half = devices // 2
    siblings = [(i, i ^ 1) for i in range(devices)]
    alike = [[2 * i + c for i in range(half)] for c in range(2)]
    prefix_of = prefix_of[:, 0]

    received = exchange(send_queries(queries, prefix_of, devices))
    suffix_out, suffix_stat = own_suffix(queries, suffix_keys, suffix_values, suffix_length)
    pack, main, tail, gates = routes(expert_index, gate_logits, devices, rows)
    back = exchange(prefix_block(received, prefix_keys, prefix_values, devices))
    attended, sent = merge(
        back, suffix_out, suffix_stat, hidden_in, norm_gain, prefix_of, pack, devices
    )
    near = exchange(sent, alike)
    far = lax.ppermute(near, "wide", siblings)
    mine, theirs = experts(near, far, gate_weight, up_weight, down_weight)
    swapped = lax.ppermute(theirs, "wide", siblings)
    parts = exchange(add_and_pack(mine, swapped), alike)
    return attended, mix(parts, main, tail, gates)


def solution(mesh):
    placed = (
        P(("groups", "wide"), None),
        P(("groups", "wide"), None),
        P(("groups", "wide"), None),
        P(("groups", "wide"), None),
        P(("groups", "wide"), None, None),
        P(("groups", "wide"), None, None),
        P(("groups", "wide")),
        P("groups", None),
        P("groups", None),
        P("groups", None),
        P(),
        P(None, "wide"),
        P(None, "wide"),
        P("wide", None),
    )
    return jax.shard_map(
        local,
        mesh=mesh,
        in_specs=placed,
        out_specs=(P(("groups", "wide"), None), P(("groups", "wide"), None)),
        check_vma=False,
    )
```

time: 172 us -> 90.6 us (0.53)
  waiting for transfers between devices: 81.4 us -> 6.09 us
  matrix products: 23.6 us -> 0 us
  Pallas kernels: 0 us -> 23.2 us
  blocking collectives: 21.3 us -> 43.6 us
  starting transfers between devices: 18 us -> 3.73 us
  between operations: 14.3 us -> 0.72 us
  local copies, waits for them, and re-layouts: 7.13 us -> 12.4 us
  other arithmetic: 5.26 us -> 0 us
    reduce_scatter x1 -> x0, waiting for transfers between devices: 56.9 us -> none  [local(): lax.psum_scatter(share[:, None] * jnp.dot(hidden_all, down_weight, prefer...]
    all_to_all x0 -> x3, blocking collectives: none -> 43.6 us  [exchange(): return lax.all_to_all(x, 'wide', 0, 0, tiled=True, axis_index_groups=groups)]
    dot_general x8 -> x0, matrix products: 23.6 us -> none  [the longest x1 12.9 us: local(): jnp.dot(hidden_all, down_weight, preferred_element_type=jnp.float32)]
    pallas_call x0 -> x8, Pallas kernels: none -> 23.2 us  [call(): pl.pallas_call(kernel, out_shape=outs, in_specs=specs, out_specs=out_spec...]
    all_to_all x4 -> x1, waiting for transfers between devices: 24.4 us -> 2.14 us  [exchange(): return lax.all_to_all(x, 'wide', 0, 0, tiled=True, axis_index_groups=groups)]
    all_gather x1 -> x0, blocking collectives: 21.3 us -> none  [local(): piece = lax.all_gather(normed, 'wide', axis=0, tiled=True)]
    all_to_all x4 -> x1, starting transfers between devices: 18 us -> 3.53 us  [exchange(): return lax.all_to_all(x, 'wide', 0, 0, tiled=True, axis_index_groups=groups)]
    unnamed x21 -> x32, local copies, waits for them, and re-layouts: 0.14 us -> 12.4 us
  transfers between devices with their start and end apart: 5 -> 3, of which waited for: 5 -> 3; matrix products, arithmetic and copies ran while one was open for 5% -> 0% of each run, Pallas kernels for 0% -> 3%
where the time goes in v2:
time: 90.6 us; the launch traced here: 89.7 us
  blocking collectives  43.6 us (48%)
  Pallas kernels  23.2 us (26%)
  local copies, waits for them, and re-layouts  12.4 us (14%)
  waiting for transfers between devices  6.09 us (7%)
  starting transfers between devices  3.73 us (4%)
    all_to_all x3, blocking collectives, exchange(): return lax.all_to_all(x, 'wide', 0, 0, tiled=True, axis_index_groups=groups)  43.6 us
    pallas_call x8, Pallas kernels, call(): pl.pallas_call(kernel, out_shape=outs, in_specs=specs, out_specs=out_spec...  23.2 us
    unnamed x32, local copies, waits for them, and re-layouts  12.4 us
    all_to_all x1, starting transfers between devices, exchange(): return lax.all_to_all(x, 'wide', 0, 0, tiled=True, axis_index_groups=groups)  3.53 us
    ppermute x1, waiting for transfers between devices, local(): swapped = lax.ppermute(theirs, 'wide', siblings)  2.36 us
    all_to_all x1, waiting for transfers between devices, exchange(): return lax.all_to_all(x, 'wide', 0, 0, tiled=True, axis_index_groups=groups)  2.14 us
  transfers between devices with their start and end apart: 3, of which 3 were waited for; matrix products, arithmetic and copies ran while one was open for 0% of the time, Pallas kernels for 3%

profile of v2, /device:TPU:0, one launch (start us, length us, event | category | flops | bytes accessed | tf_op | source)
XLA Modules:
  0.0 89.7 jit_solution(18003304301025273328)
XLA Ops:
  0.6 0.0 copy-start.3
  0.6 0.8 copy-done.3
  1.4 0.0 copy-start.7
  1.4 0.7 copy-done.7
  2.1 0.8 shard_map.149
  2.8 16.2 %all_to_all.44 = bf16[16,8,768]{2,1,0:T(8,128)(2,1)S(1)} all-to-all(bf16[16,8,768]{2,1,0:T(8,128)(2,1)S(1)} %bitcast.17), channel_id=1, replica_groups=mesh['groups'=2,'wide'=16] {'wide'}, dimensions={0} | all-to-all | bytes 393216 | tf_op jit(solution)/shard_map/all_to_all | solution.py:465
  19.0 0.0 copy-start.1
  19.0 1.0 %copy-done.1 = bf16[512,512]{1,0:T(8,128)(2,1)S(1)} copy-done((bf16[512,512]{1,0:T(8,128)(2,1)S(1)}, bf16[512,512]{1,0:T(8,128)(2,1)}, u32[]{:S(2)}) %copy-start.1) | copy-done | bytes 524312
  20.1 0.0 copy-start.2
  20.1 1.0 %copy-done.2 = bf16[512,512]{1,0:T(8,128)(2,1)S(1)} copy-done((bf16[512,512]{1,0:T(8,128)(2,1)S(1)}, bf16[512,512]{1,0:T(8,128)(2,1)}, u32[]{:S(2)}) %copy-start.2) | copy-done | bytes 524312
  21.1 2.3 %shard_map.150 = bf16[128,896]{1,0:T(8,128)(2,1)} custom-call(bf16[128,768]{1,0:T(8,128)(2,1)S(1)} %bitcast.18, bf16[512,512]{1,0:T(8,128)(2,1)S(1)} %copy-done.1, bf16[512,512]{1,0:T(8,128)(2,1)S(1)} %copy-done.2), custom_call_target="tpu_custom_call" | custom-call | bytes 1048576 | tf_op jit(solution)/shard_map/pallas_call | solution.py:80
  23.4 3.5 %all-to-all-start.1 = ((bf16[16,8,896]{2,1,0:T(8,128)(2,1)}), bf16[16,8,896]{2,1,0:T(8,128)(2,1)S(1)}, u32[]{:S(2)}, u32[]{:S(2)}) async-start(bf16[16,8,896]{2,1,0:T(8,128)(2,1)} %bitcast.3), calls=%async_computation.1 | async-start | bytes 458752 | tf_op jit(solution)/shard_map/all_to_all | solution.py:465
  26.9 0.0 copy-start.11
  26.9 0.7 copy-done.11
  27.6 0.0 copy-start.12
  27.6 0.7 copy-done.12
  28.3 0.7 shard_map.152
  29.0 0.0 copy-start.4
  29.0 0.8 copy-done.4
  29.8 0.0 copy-start.9
  29.8 1.0 %copy-done.9 = bf16[8,64,512]{2,1,0:T(8,128)(2,1)S(1)} copy-done((bf16[8,64,512]{2,1,0:T(8,128)(2,1)S(1)}, bf16[8,64,512]{2,1,0:T(8,128)(2,1)}, u32[]{:S(2)}) %copy-start.9) | copy-done | bytes 524312
  30.9 0.0 copy-start.10
  30.9 1.0 %copy-done.10 = bf16[8,64,512]{2,1,0:T(8,128)(2,1)S(1)} copy-done((bf16[8,64,512]{2,1,0:T(8,128)(2,1)S(1)}, bf16[8,64,512]{2,1,0:T(8,128)(2,1)}, u32[]{:S(2)}) %copy-start.10) | copy-done | bytes 524312
  31.9 0.0 copy-start.13
  31.9 0.7 copy-done.13
  32.6 1.7 %shard_map.151 = (f32[32,768]{1,0:T(8,128)S(1)}, f32[32,128]{1,0:T(8,128)S(1)}) custom-call(bf16[8,3072]{1,0:T(8,128)(2,1)S(1)} %copy-done.4, bf16[512,512]{1,0:T(8,128)(2,1)S(1)} %bitcast.23, bf16[512,512]{1,0:T(8,128)(2,1)S(1)} %bitcast.24, s32[8]{0:T(128)S(1)} %copy-done.13), custom_call_target="tpu_custom_call" | custom-call | flops 536870912 | bytes 1048576 | tf_op jit(solution)/shard_map/pallas_call | solution.py:80
  34.2 2.1 %all-to-all-done.1 = bf16[16,8,896]{2,1,0:T(8,128)(2,1)S(1)} async-done(((bf16[16,8,896]{2,1,0:T(8,128)(2,1)}), bf16[16,8,896]{2,1,0:T(8,128)(2,1)S(1)}, u32[]{:S(2)}, u32[]{:S(2)}) %all-to-all-start.1) | async-done | bytes 229408 | tf_op jit(solution)/shard_map/all_to_all | solution.py:465
  36.4 0.0 copy-start.5
  36.4 0.8 copy-done.5
  37.2 0.0 copy-start.6
  37.2 0.7 copy-done.6
  37.9 0.0 copy-start.8
  37.9 0.7 copy-done.8
  38.5 1.7 %shard_map.153 = (bf16[8,3072]{1,0:T(8,128)(2,1)}, bf16[64,2304]{1,0:T(8,128)(2,1)S(1)}) custom-call(bf16[128,896]{1,0:T(8,128)(2,1)S(1)} %bitcast.16, f32[32,768]{1,0:T(8,128)S(1)} %get-tuple-element.12.suffix_ref, f32[32,128]{1,0:T(8,128)S(1)} %get-tuple-element.13.stat_ref, bf16[8,3072]{1,0:T(8,128)(2,1)S(1)} %copy-done.5, f32[1,3072]{1,0:T(1,128)S(1)} %bitcast.20, ...), custom_call_target="tpu_custom_call" | custom-call | bytes 1048576 | tf_op jit(solution)/shard_map/pallas_call | solution.py:80
  40.2 14.1 %all_to_all.45 = bf16[8,8,2304]{2,1,0:T(8,128)(2,1)S(1)} all-to-all(bf16[8,8,2304]{2,1,0:T(8,128)(2,1)S(1)} %bitcast.19), channel_id=1, replica_groups={{0,2,4,6,8,10,12,14},{1,3,5,7,9,11,13,15},{16,18,20,22,24,26,28,30},{17..., dimensions={0} | all-to-all | bytes 589824 | tf_op jit(solution)/shard_map/all_to_all | solution.py:465
  54.4 0.0 collective-permute-start
  54.4 1.6 %collective-permute-done.far_ref = bf16[64,2304]{1,0:T(8,128)(2,1)S(1)} collective-permute-done((bf16[64,2304]{1,0:T(8,128)(2,1)S(1)}, bf16[64,2304]{1,0:T(8,128)(2,1)S(1)}, u32[]{:S(2)}, u32[]{:S(2)}) %collective-permute-start) | collective-permute-done | bytes 294944 | tf_op jit(solution)/shard_map/ppermute | solution.py:499
  55.9 0.0 copy-done.14
  55.9 0.0 copy-start.15
  56.0 0.7 copy-done.15
  56.7 15.0 %shard_map.154 = (f32[64,3072]{1,0:T(8,128)}, f32[64,3072]{1,0:T(8,128)}) custom-call(bf16[64,2304]{1,0:T(8,128)(2,1)} %bitcast.28, bf16[64,2304]{1,0:T(8,128)(2,1)} %copy-done.15, bf16[3072,2048]{1,0:T(8,128)(2,1)} %gate_hbm.1, bf16[3072,2048]{1,0:T(8,128)(2,1)} %up_hbm.1, bf16[2048,3072]{1,0:T(8,128)(2,1)} %down_hbm.1), custom_call_target="tpu_custom_call" | custom-call | flops 4831838208 | bytes 37748736 | tf_op jit(solution)/shard_map/pallas_call | solution.py:80
  71.7 0.2 collective-permute-start.1
  71.9 2.4 %collective-permute-done.1.swapped_ref = f32[64,3072]{1,0:T(8,128)S(1)} collective-permute-done((f32[64,3072]{1,0:T(8,128)}, f32[64,3072]{1,0:T(8,128)S(1)}, u32[]{:S(2)}, u32[]{:S(2)}) %collective-permute-start.1) | collective-permute-done | bytes 786464 | tf_op jit(solution)/shard_map/ppermute | solution.py:501
  74.3 0.0 copy-start
  74.3 1.1 %copy-done = f32[64,3072]{1,0:T(8,128)S(1)} copy-done((f32[64,3072]{1,0:T(8,128)S(1)}, f32[64,3072]{1,0:T(8,128)}, u32[]{:S(2)}) %copy-start) | copy-done | bytes 786456
  75.4 0.2 shard_map.155
  75.6 13.3 %all_to_all.46 = bf16[8,8,2304]{2,1,0:T(8,128)(2,1)S(1)} all-to-all(bf16[8,8,2304]{2,1,0:T(8,128)(2,1)S(1)} %bitcast.14), channel_id=1, replica_groups={{0,2,4,6,8,10,12,14},{1,3,5,7,9,11,13,15},{16,18,20,22,24,26,28,30},{17..., dimensions={0} | all-to-all | bytes 589824 | tf_op jit(solution)/shard_map/all_to_all | solution.py:465
  88.9 0.8 shard_map.156
  (1 shorter events, 0.0 us)
Async XLA Ops:
  0.6 0.8 copy-start.3
  1.4 0.7 copy-start.7
  19.0 1.0 %copy-start.1 = (bf16[512,512]{1,0:T(8,128)(2,1)S(1)}, bf16[512,512]{1,0:T(8,128)(2,1)}, u32[]{:S(2)}) copy-start(bf16[512,512]{1,0:T(8,128)(2,1)} %key_ref.1) | copy-start | bytes 1572868
  20.1 1.0 %copy-start.2 = (bf16[512,512]{1,0:T(8,128)(2,1)S(1)}, bf16[512,512]{1,0:T(8,128)(2,1)}, u32[]{:S(2)}) copy-start(bf16[512,512]{1,0:T(8,128)(2,1)} %value_ref.1) | copy-start | bytes 1572868
  23.4 13.0 %all-to-all-start.1 = ((bf16[16,8,896]{2,1,0:T(8,128)(2,1)}), bf16[16,8,896]{2,1,0:T(8,128)(2,1)S(1)}, u32[]{:S(2)}, u32[]{:S(2)}) async-start(bf16[16,8,896]{2,1,0:T(8,128)(2,1)} %bitcast.3), calls=%async_computation.1 | async-start | bytes 458752 | tf_op jit(solution)/shard_map/all_to_all | solution.py:465
  26.9 0.7 copy-start.11
  27.6 0.7 copy-start.12
  29.0 0.8 copy-start.4
  29.8 1.0 %copy-start.9 = (bf16[8,64,512]{2,1,0:T(8,128)(2,1)S(1)}, bf16[8,64,512]{2,1,0:T(8,128)(2,1)}, u32[]{:S(2)}) copy-start(bf16[8,64,512]{2,1,0:T(8,128)(2,1)} %param.18) | copy-start | bytes 1572868
  30.9 1.0 %copy-start.10 = (bf16[8,64,512]{2,1,0:T(8,128)(2,1)S(1)}, bf16[8,64,512]{2,1,0:T(8,128)(2,1)}, u32[]{:S(2)}) copy-start(bf16[8,64,512]{2,1,0:T(8,128)(2,1)} %param.19) | copy-start | bytes 1572868
  31.9 0.7 copy-start.13
  36.4 0.8 copy-start.5
  37.2 0.7 copy-start.6
  37.9 0.7 copy-start.8
  54.4 1.6 %copy-start.14 = (bf16[8,8,2304]{2,1,0:T(8,128)(2,1)}, bf16[8,8,2304]{2,1,0:T(8,128)(2,1)S(1)}, u32[]{:S(2)}) copy-start(bf16[8,8,2304]{2,1,0:T(8,128)(2,1)S(1)} %all_to_all.45) | copy-start | bytes 884740
  54.4 1.6 %collective-permute-start = (bf16[64,2304]{1,0:T(8,128)(2,1)S(1)}, bf16[64,2304]{1,0:T(8,128)(2,1)S(1)}, u32[]{:S(2)}, u32[]{:S(2)}) collective-permute-start(bf16[64,2304]{1,0:T(8,128)(2,1)S(1)} %bitcast.27), channel_id=1, source_target_pairs={{0,1},{1,0},{2,3},{3,2},{4,5},{5,4},{6,7},{7,6},{8,9},{9,8},{10,11... | collective-permute-start | bytes 884744 | tf_op jit(solution)/shard_map/ppermute | solution.py:499
  55.9 0.7 copy-start.15
  71.7 2.6 %collective-permute-start.1 = (f32[64,3072]{1,0:T(8,128)}, f32[64,3072]{1,0:T(8,128)S(1)}, u32[]{:S(2)}, u32[]{:S(2)}) collective-permute-start(f32[64,3072]{1,0:T(8,128)} %get-tuple-element.18), channel_id=1, source_target_pairs={{0,1},{1,0},{2,3},{3,2},{4,5},{5,4},{6,7},{7,6},{8,9},{9,8},{10,11... | collective-permute-start | bytes 2359304 | tf_op jit(solution)/shard_map/ppermute | solution.py:501
  74.3 1.1 %copy-start = (f32[64,3072]{1,0:T(8,128)S(1)}, f32[64,3072]{1,0:T(8,128)}, u32[]{:S(2)}) copy-start(f32[64,3072]{1,0:T(8,128)} %get-tuple-element.17.mine_ref) | copy-start | bytes 2359300

commit v3 on v2

--- a/solution.py
+++ b/solution.py
@@ -77,6 +77,7 @@
 
 
 def call(kernel, outs, ins, specs, flops=0, limit=24, scratch=(), moved=0, out_specs=None):
+    ins = [pltpu.with_memory_space_constraint(x, pltpu.HBM) if s is HBM else x for x, s in zip(ins, specs)]
     return pl.pallas_call(
         kernel,
         out_shape=outs,
@@ -90,19 +91,29 @@
     )(*ins)
 
 
+def fetch(pairs, sems):
+    copies = [pltpu.make_async_copy(s, t, sems.at[n]) for n, (s, t) in enumerate(pairs)]
+    for copy in copies:
+        copy.start()
+    return copies
+
+
 def send_queries(queries, prefix_of, devices):
     rows = queries.shape[0]
     holders = devices // PREFIXES
 
-    def kernel(query_ref, prefix_ref, out_ref):
-        start = lax.axis_index("wide") * rows
-        named, ranks = prefix_slots(prefix_ref, start, rows)
+    def kernel(query_hbm, prefix_hbm, out_ref, query_ref, prefix_ref, sems):
+        copies = fetch([(prefix_hbm, prefix_ref), (query_hbm, query_ref)], sems)
         row, col = iotas((devices * HK * CAPP, HK * rows))
         device, k, c = div(row, HK * CAPP), mod(div(row, CAPP), HK), mod(row, CAPP)
         r = mod(col, rows)
+        copies[0].wait()
+        start = lax.axis_index("wide") * rows
+        named, ranks = prefix_slots(prefix_ref, start, rows)
         picked = (
             (k == div(col, rows)) & (div(device, holders) == by_row(r, named)) & (c == by_row(r, ranks))
         )
+        copies[1].wait()
         pieces = stack_pieces(query_ref[...].astype(F32)).astype(BF16)
         out_ref[...] = dot(one_hot(picked), pieces).astype(BF16)
 
@@ -110,7 +121,13 @@
         kernel,
         jax.ShapeDtypeStruct((devices * HK * CAPP, PIECE), BF16),
         (queries, prefix_of),
-        [VMEM, SMEM],
+        [HBM, HBM],
+        scratch=[
+            pltpu.VMEM(queries.shape, BF16),
+            pltpu.SMEM(prefix_of.shape, jnp.int32),
+            pltpu.SemaphoreType.DMA((2,)),
+        ],
+        limit=4,
     )
 
 
@@ -128,45 +145,30 @@
     return jnp.concatenate([x[:, g * DH : (g + 1) * DH] for g in range(GROUP)], axis=0)
 
 
-def own_suffix(queries, keys, values, lengths):
-    rows = queries.shape[0]
-    span = keys.shape[1]
-    flat = (rows * span, keys.shape[2])
-
-    def kernel(query_ref, key_ref, value_ref, length_ref, out_ref, stat_ref):
-        row, col = iotas((rows, rows * span))
-        owner = div(col, span)
-        live = (owner == row) & (mod(col, span) < by_row(owner, [length_ref[r] for r in range(rows)]))
-        mask = jnp.concatenate([live.astype(F32)] * GROUP, axis=0) > 0.5
-        lane = iotas((rows, STAT))[1]
-        query = query_ref[...].astype(F32)
-        for k in range(HK):
-            cols = pl.ds(k * DH, DH)
-            own = pl.ds(k * rows, rows)
-            out, top, total = softmax_block(
-                heads_of(query[:, k * PIECE : (k + 1) * PIECE]).astype(BF16),
-                key_ref[:, cols],
-                value_ref[:, cols],
-                mask,
-            )
-            stat = jnp.zeros((rows, STAT), F32)
-            for g in range(GROUP):
-                part = slice(g * rows, (g + 1) * rows)
-                out_ref[own, pl.ds(g * DH, DH)] = out[part]
-                stat = jnp.where(lane == g, top[part], stat)
-                stat = jnp.where(lane == SLOT + g, total[part], stat)
-            stat_ref[own, :] = stat
-
-    return call(
-        kernel,
-        (
-            jax.ShapeDtypeStruct((HK * rows, PIECE), F32),
-            jax.ShapeDtypeStruct((HK * rows, STAT), F32),
-        ),
-        (queries, keys.reshape(flat), values.reshape(flat), lengths),
-        [VMEM, VMEM, VMEM, SMEM],
-        flops=1 << 29,
-    )
+def own_suffix(query, key_ref, value_ref, lengths, out_ref, stat_ref):
+    rows = query.shape[0]
+    span = key_ref.shape[0] // rows
+    row, col = iotas((rows, rows * span))
+    owner = div(col, span)
+    live = (owner == row) & (mod(col, span) < by_row(owner, lengths))
+    mask = jnp.concatenate([live.astype(F32)] * GROUP, axis=0) > 0.5
+    lane = iotas((rows, STAT))[1]
+    for k in range(HK):
+        cols = pl.ds(k * DH, DH)
+        own = pl.ds(k * rows, rows)
+        out, top, total = softmax_block(
+            heads_of(query[:, k * PIECE : (k + 1) * PIECE]).astype(BF16),
+            key_ref[:, cols],
+            value_ref[:, cols],
+            mask,
+        )
+        stat = jnp.zeros((rows, STAT), F32)
+        for g in range(GROUP):
+            part = slice(g * rows, (g + 1) * rows)
+            out_ref[own, pl.ds(g * DH, DH)] = out[part]
+            stat = jnp.where(lane == g, top[part], stat)
+            stat = jnp.where(lane == SLOT + g, total[part], stat)
+        stat_ref[own, :] = stat
 
 
 def prefix_block(received, keys, values, devices):
@@ -208,84 +210,144 @@
         jax.ShapeDtypeStruct((total_rows, PIECE + STAT), BF16),
         (received, keys, values),
         [VMEM, VMEM, VMEM],
-    )
-
-
-def routes(expert_index, gate_logits, devices, rows):
+        limit=8,
+    )
+
+
+def routes(named, logits, half, pack_ref, main_ref, tail_ref, gate_ref):
+    rows = len(named[0])
+    per_expert = half // EXPERTS
+    row, col = iotas((EXPERTS * SLOT, HK * rows))
+    expert, i, k, r = div(row, SLOT), mod(row, SLOT), div(col, rows), mod(col, rows)
+    has = (by_row(r, named[0]) == expert) | (by_row(r, named[1]) == expert)
+    a, b = iotas((HK * rows, HK * rows))
+    earlier = (div(a, rows) == div(b, rows)) & (mod(a, rows) < mod(b, rows))
+    rank = dot(one_hot(has), one_hot(earlier)).astype(jnp.int32)
+    for n in range(BLOCKS):
+        slot = jnp.where(i < CAPE, i, (i - CAPE) * PER + n)
+        piece = jnp.where(i < CAPE, n, HK - 1)
+        pack_ref[n] = one_hot(has & (rank == slot) & (k == piece))
+
+    row, col = iotas((2 * rows, half * SLOT))
+    j, r = div(row, rows), mod(row, rows)
+    expert, i = div(div(col, SLOT), per_expert), mod(col, SLOT)
+    mine = jnp.where(j == 0, by_row(r, named[0]), by_row(r, named[1]))
+    rank = jnp.zeros(row.shape, jnp.int32)
+    for q in range(rows):
+        same = (mine == named[0][q]) | (mine == named[1][q])
+        rank += ((r > q) & same).astype(jnp.int32)
+    here = expert == mine
+    main_ref[...] = one_hot(here & (i == rank))
+    for n in range(BLOCKS):
+        spot = jnp.full(row.shape, -1, jnp.int32)
+        for m in range(SLOT - CAPE):
+            spot = jnp.where(rank == m * PER + n, CAPE + m, spot)
+        tail_ref[n] = one_hot(here & (i == spot))
+
+    row, _ = iotas((rows, STAT))
+    first, second = by_row(row, logits[0]), by_row(row, logits[1])
+    top = jnp.maximum(first, second)
+    first, second = jnp.exp(first - top), jnp.exp(second - top)
+    gate_ref[0] = first / (first + second)
+    gate_ref[1] = second / (first + second)
+
+
+def prepare(
+    queries, suffix_keys, suffix_values, lengths, prefix_of, expert_index, gate_logits,
+    keys, values, hidden_in, norm_gain, devices,
+):
+    rows = queries.shape[0]
+    half = devices // 2
+    holders = devices // PREFIXES
+    flat = (rows * suffix_keys.shape[1], suffix_keys.shape[2])
+    gain = norm_gain.reshape(1, norm_gain.shape[0])
+    expert_index, gate_logits = expert_index.T, gate_logits.T
+
+    def kernel(
+        query_hbm, skey_hbm, svalue_hbm, length_hbm, prefix_hbm, expert_hbm, logit_hbm,
+        key_hbm, value_hbm, hidden_hbm, gain_hbm,
+        suffix_ref, stat_ref, pack_ref, main_ref, tail_ref, gate_ref, find_ref,
+        key_ref, value_ref, hidden_ref, gain_ref,
+        query_ref, skey_ref, svalue_ref, length_ref, prefix_ref, expert_ref, logit_ref, sems,
+    ):
+        copies = fetch(
+            [
+                (expert_hbm, expert_ref), (logit_hbm, logit_ref), (prefix_hbm, prefix_ref),
+                (length_hbm, length_ref), (query_hbm, query_ref), (skey_hbm, skey_ref),
+                (svalue_hbm, svalue_ref), (key_hbm, key_ref), (value_hbm, value_ref),
+                (hidden_hbm, hidden_ref), (gain_hbm, gain_ref),
+            ],
+            sems,
+        )
+        start = lax.axis_index("wide") * rows
+        for copy in copies[:3]:
+            copy.wait()
+        named = [[expert_ref[j, start + r] for r in range(rows)] for j in range(2)]
+        logits = [[logit_ref[j, start + r] for r in range(rows)] for j in range(2)]
+        routes(named, logits, half, pack_ref, main_ref, tail_ref, gate_ref)
+
+        named, ranks = prefix_slots(prefix_ref, start, rows)
+        firsts = [named[r] * (holders * HK * CAPP) + ranks[r] for r in range(rows)]
+        row, col = iotas((HK * rows, devices * HK * CAPP))
+        target = by_row(mod(row, rows), firsts) + div(row, rows) * CAPP
+        for h in range(holders):
+            find_ref[h] = one_hot(target + h * (HK * CAPP) == col)
+
+        for copy in copies[3:7]:
+            copy.wait()
+        lengths = [length_ref[r] for r in range(rows)]
+        own_suffix(query_ref[...].astype(F32), skey_ref, svalue_ref, lengths, suffix_ref, stat_ref)
+        for copy in copies[7:]:
+            copy.wait()
+
+    shape = jax.ShapeDtypeStruct
+    return call(
+        kernel,
+        (
+            shape((HK * rows, PIECE), F32),
+            shape((HK * rows, STAT), F32),
+            shape((BLOCKS, EXPERTS * SLOT, HK * rows), BF16),
+            shape((2 * rows, half * SLOT), BF16),
+            shape((BLOCKS, 2 * rows, half * SLOT), BF16),
+            shape((2, rows, STAT), F32),
+            shape((holders, HK * rows, devices * HK * CAPP), BF16),
+            shape(keys.shape, BF16),
+            shape(values.shape, BF16),
+            shape(hidden_in.shape, BF16),
+            shape(gain.shape, F32),
+        ),
+        (
+            queries, suffix_keys.reshape(flat), suffix_values.reshape(flat), lengths, prefix_of,
+            expert_index, gate_logits, keys, values, hidden_in, gain,
+        ),
+        [HBM] * 11,
+        flops=1 << 31,
+        scratch=[
+            pltpu.VMEM(queries.shape, BF16),
+            pltpu.VMEM(flat, BF16),
+            pltpu.VMEM(flat, BF16),
+            pltpu.SMEM(lengths.shape, jnp.int32),
+            pltpu.SMEM(prefix_of.shape, jnp.int32),
+            pltpu.SMEM(expert_index.shape, jnp.int32),
+            pltpu.SMEM(gate_logits.shape, F32),
+            pltpu.SemaphoreType.DMA((11,)),
+        ],
+        limit=8,
+    )
+
+
+def merge(back, suffix_out, suffix_stat, hidden_in, gain, find, pack, devices):
+    rows, width = hidden_in.shape
     half = devices // 2
     per_expert = half // EXPERTS
 
-    def kernel(expert_ref, logit_ref, pack_ref, main_ref, tail_ref, gate_ref):
-        start = lax.axis_index("wide") * rows
-        named = [[expert_ref[j, start + r] for r in range(rows)] for j in range(2)]
-        logits = [[logit_ref[j, start + r] for r in range(rows)] for j in range(2)]
-
-        row, col = iotas((EXPERTS * SLOT, HK * rows))
-        expert, i, k, r = div(row, SLOT), mod(row, SLOT), div(col, rows), mod(col, rows)
-        has = (by_row(r, named[0]) == expert) | (by_row(r, named[1]) == expert)
-        a, b = iotas((HK * rows, HK * rows))
-        earlier = (div(a, rows) == div(b, rows)) & (mod(a, rows) < mod(b, rows))
-        rank = dot(one_hot(has), one_hot(earlier)).astype(jnp.int32)
-        for n in range(BLOCKS):
-            slot = jnp.where(i < CAPE, i, (i - CAPE) * PER + n)
-            piece = jnp.where(i < CAPE, n, HK - 1)
-            pack_ref[n] = one_hot(has & (rank == slot) & (k == piece))
-
-        row, col = iotas((2 * rows, half * SLOT))
-        j, r = div(row, rows), mod(row, rows)
-        expert, i = div(div(col, SLOT), per_expert), mod(col, SLOT)
-        mine = jnp.where(j == 0, by_row(r, named[0]), by_row(r, named[1]))
-        rank = jnp.zeros(row.shape, jnp.int32)
-        for q in range(rows):
-            same = (mine == named[0][q]) | (mine == named[1][q])
-            rank += ((r > q) & same).astype(jnp.int32)
-        here = expert == mine
-        main_ref[...] = one_hot(here & (i == rank))
-        for n in range(BLOCKS):
-            spot = jnp.full(row.shape, -1, jnp.int32)
-            for m in range(SLOT - CAPE):
-                spot = jnp.where(rank == m * PER + n, CAPE + m, spot)
-            tail_ref[n] = one_hot(here & (i == spot))
-
-        row, _ = iotas((rows, STAT))
-        first, second = by_row(row, logits[0]), by_row(row, logits[1])
-        top = jnp.maximum(first, second)
-        first, second = jnp.exp(first - top), jnp.exp(second - top)
-        gate_ref[0] = first / (first + second)
-        gate_ref[1] = second / (first + second)
-
-    return call(
-        kernel,
-        (
-            jax.ShapeDtypeStruct((BLOCKS, EXPERTS * SLOT, HK * rows), BF16),
-            jax.ShapeDtypeStruct((2 * rows, half * SLOT), BF16),
-            jax.ShapeDtypeStruct((BLOCKS, 2 * rows, half * SLOT), BF16),
-            jax.ShapeDtypeStruct((2, rows, STAT), F32),
-        ),
-        (expert_index.T, gate_logits.T),
-        [SMEM, SMEM],
-        flops=1 << 29,
-    )
-
-
-def merge(back, suffix_out, suffix_stat, hidden_in, norm_gain, prefix_of, pack, devices):
-    rows, width = hidden_in.shape
-    holders = devices // PREFIXES
-    half = devices // 2
-    per_expert = half // EXPERTS
-
     def kernel(
-        back_ref, suffix_ref, stat_ref, hidden_ref, gain_ref, prefix_ref, pack_ref, out_ref, sent_ref
+        back_ref, suffix_ref, stat_ref, hidden_ref, gain_ref, find_ref, pack_ref, out_ref, sent_ref
     ):
-        start = lax.axis_index("wide") * rows
-        named, ranks = prefix_slots(prefix_ref, start, rows)
-        firsts = [named[r] * (holders * HK * CAPP) + ranks[r] for r in range(rows)]
-        row, col = iotas((HK * rows, back_ref.shape[0]))
-        target = by_row(mod(row, rows), firsts) + div(row, rows) * CAPP
         stat = stat_ref[...]
         outs, tops, sums = [suffix_ref[...]], [stat[:, :SLOT]], [stat[:, SLOT : 2 * SLOT]]
-        for h in range(holders):
-            found = dot(one_hot(target + h * (HK * CAPP) == col), back_ref[...])
+        for h in range(find_ref.shape[0]):
+            found = dot(find_ref[h], back_ref[...])
             stat = found[:, PIECE:]
             field = [stat[:, n * SLOT : (n + 1) * SLOT] for n in range(5)]
             outs.append(found[:, :PIECE])
@@ -330,8 +392,9 @@
             jax.ShapeDtypeStruct((rows, width), BF16),
             jax.ShapeDtypeStruct((half * SLOT, BLOCKS * PIECE), BF16),
         ),
-        (back, suffix_out, suffix_stat, hidden_in, norm_gain.reshape(1, width), prefix_of, pack),
-        [VMEM, VMEM, VMEM, VMEM, VMEM, SMEM, VMEM],
+        (back, suffix_out, suffix_stat, hidden_in, gain, find, pack),
+        [VMEM] * 7,
+        limit=8,
     )
 
 
@@ -404,7 +467,7 @@
         [VMEM, VMEM, HBM, HBM, HBM],
         flops=12 * half * units * width,
         moved=6 * units * width,
-        limit=56,
+        limit=42,
         scratch=[
             pltpu.VMEM(gate_weight.shape, BF16),
             pltpu.VMEM(up_weight.shape, BF16),
@@ -488,13 +551,15 @@
     alike = [[2 * i + c for i in range(half)] for c in range(2)]
     prefix_of = prefix_of[:, 0]
 
-    received = exchange(send_queries(queries, prefix_of, devices))
-    suffix_out, suffix_stat = own_suffix(queries, suffix_keys, suffix_values, suffix_length)
-    pack, main, tail, gates = routes(expert_index, gate_logits, devices, rows)
-    back = exchange(prefix_block(received, prefix_keys, prefix_values, devices))
-    attended, sent = merge(
-        back, suffix_out, suffix_stat, hidden_in, norm_gain, prefix_of, pack, devices
-    )
+    outgoing = send_queries(queries, prefix_of, devices)
+    outgoing, suffix_length = lax.optimization_barrier((outgoing, suffix_length))
+    received = exchange(outgoing)
+    suffix_out, suffix_stat, pack, main, tail, gates, find, keys, values, hidden, gain = prepare(
+        queries, suffix_keys, suffix_values, suffix_length, prefix_of, expert_index, gate_logits,
+        prefix_keys, prefix_values, hidden_in, norm_gain, devices,
+    )
+    back = exchange(prefix_block(received, keys, values, devices))
+    attended, sent = merge(back, suffix_out, suffix_stat, hidden, gain, find, pack, devices)
     near = exchange(sent, alike)
     far = lax.ppermute(near, "wide", siblings)
     mine, theirs = experts(near, far, gate_weight, up_weight, down_weight)

time: 90.6 us -> 78.1 us (0.86)
  local copies, waits for them, and re-layouts: 12.4 us -> 0 us
  blocking collectives: 43.6 us -> 38.5 us
  waiting for transfers between devices: 6.09 us -> 10.2 us
  starting transfers between devices: 3.73 us -> 7.63 us
  Pallas kernels: 23.2 us -> 20.7 us
    unnamed x32 -> x0, local copies, waits for them, and re-layouts: 12.4 us -> none
    all_to_all x3, blocking collectives: 43.6 us -> 38.5 us  [exchange(): return lax.all_to_all(x, 'wide', 0, 0, tiled=True, axis_index_groups=groups)]
    all_to_all x1, waiting for transfers between devices: 2.14 us -> 6.48 us  [exchange(): return lax.all_to_all(x, 'wide', 0, 0, tiled=True, axis_index_groups=groups)]
    all_to_all x1, starting transfers between devices: 3.53 us -> 7.43 us  [exchange(): return lax.all_to_all(x, 'wide', 0, 0, tiled=True, axis_index_groups=groups)]
    pallas_call x8 -> x7, Pallas kernels: 23.2 us -> 20.7 us  [call(): pl.pallas_call(kernel, out_shape=outs, in_specs=specs, out_specs=out_spec...]
where the time goes in v3:
time: 78.1 us; the launch traced here: 77.7 us
  blocking collectives  38.5 us (49%)
  Pallas kernels  20.7 us (27%)
  waiting for transfers between devices  10.2 us (13%)
  starting transfers between devices  7.63 us (10%)
    all_to_all x3, blocking collectives, exchange(): return lax.all_to_all(x, 'wide', 0, 0, tiled=True, axis_index_groups=groups)  38.5 us
    pallas_call x7, Pallas kernels, call(): pl.pallas_call(kernel, out_shape=outs, in_specs=specs, out_specs=out_spec...  20.7 us
    all_to_all x1, starting transfers between devices, exchange(): return lax.all_to_all(x, 'wide', 0, 0, tiled=True, axis_index_groups=groups)  7.43 us
    all_to_all x1, waiting for transfers between devices, exchange(): return lax.all_to_all(x, 'wide', 0, 0, tiled=True, axis_index_groups=groups)  6.48 us
    ppermute x1, waiting for transfers between devices, local(): swapped = lax.ppermute(theirs, 'wide', siblings)  2.15 us
    ppermute x1, waiting for transfers between devices, local(): far = lax.ppermute(near, 'wide', siblings)  1.58 us
  transfers between devices with their start and end apart: 3, of which 3 were waited for; matrix products, arithmetic and copies ran while one was open for 0% of the time, Pallas kernels for 3%

profile of v3, /device:TPU:0, one launch (start us, length us, event | category | flops | bytes accessed | tf_op | source)
XLA Modules:
  0.0 77.7 jit_solution(12485123535513289633)
XLA Ops:
  0.6 1.7 %shard_map.149 = bf16[128,768]{1,0:T(8,128)(2,1)} custom-call(bf16[8,3072]{1,0:T(8,128)(2,1)} %query_hbm.3, s32[128]{0:T(128)} %bitcast.22), custom_call_target="tpu_custom_call" | custom-call | bytes 1048576 | tf_op jit(solution)/shard_map/pallas_call | solution.py:81
  2.3 7.4 %all-to-all-start = ((bf16[16,8,768]{2,1,0:T(8,128)(2,1)}), bf16[16,8,768]{2,1,0:T(8,128)(2,1)S(1)}, u32[]{:S(2)}, u32[]{:S(2)}) async-start(bf16[16,8,768]{2,1,0:T(8,128)(2,1)} %bitcast.1), calls=%async_computation | async-start | bytes 393216 | tf_op jit(solution)/shard_map/all_to_all | solution.py:528
  9.7 2.5 %shard_map.150 = (f32[32,768]{1,0:T(8,128)S(1)}, f32[32,128]{1,0:T(8,128)S(1)}, bf16[3,32,32]{2,1,0:T(8,128)(2,1)S(1)}, bf16[16,64]{1,0:T(8,128)(2,1)S(1)}, bf16...) custom-call(bf16[8,3072]{1,0:T(8,128)(2,1)} %query_hbm.3, ...), custom_call_target="tpu_custom_call" | custom-call | flops 2147483648 | bytes 1048576 | tf_op jit(solution)/shard_map/pallas_call | solution.py:81
  12.2 6.5 %all-to-all-done = bf16[16,8,768]{2,1,0:T(8,128)(2,1)S(1)} async-done(((bf16[16,8,768]{2,1,0:T(8,128)(2,1)}), bf16[16,8,768]{2,1,0:T(8,128)(2,1)S(1)}, u32[]{:S(2)}, u32[]{:S(2)}) %all-to-all-start) | async-done | bytes 196640 | tf_op jit(solution)/shard_map/all_to_all | solution.py:528
  18.7 1.6 %shard_map.151 = bf16[128,896]{1,0:T(8,128)(2,1)S(1)} custom-call(bf16[128,768]{1,0:T(8,128)(2,1)S(1)} %bitcast.20, bf16[512,512]{1,0:T(8,128)(2,1)S(1)} %get-tuple-element.21.key_ref, bf16[512,512]{1,0:T(8,128)(2,1)S(1)} %get-tuple-element.22.value_ref), custom_call_target="tpu_custom_call" | custom-call | bytes 1048576 | tf_op jit(solution)/shard_map/pallas_call | solution.py:81
  20.3 12.1 %all_to_all.44 = bf16[16,8,896]{2,1,0:T(8,128)(2,1)S(1)} all-to-all(bf16[16,8,896]{2,1,0:T(8,128)(2,1)S(1)} %bitcast.19), channel_id=1, replica_groups=mesh['groups'=2,'wide'=16] {'wide'}, dimensions={0} | all-to-all | bytes 458752 | tf_op jit(solution)/shard_map/all_to_all | solution.py:528
  32.4 1.1 %shard_map.152 = (bf16[8,3072]{1,0:T(8,128)(2,1)}, bf16[64,2304]{1,0:T(8,128)(2,1)S(1)}) custom-call(bf16[128,896]{1,0:T(8,128)(2,1)S(1)} %bitcast.18, f32[32,768]{1,0:T(8,128)S(1)} %get-tuple-element.23.suffix_ref, f32[32,128]{1,0:T(8,128)S(1)} %get-tuple-element.24.stat_ref, bf16[8,3072]{1,0:T(8,128)(2,1)S(1)} %get-tuple-element.25.hidden_ref, ...), custom_call_target="tpu_custom_call" | custom-call | bytes 1048576 | tf_op jit(solution)/shard_map/pallas_call | solution.py:81
  33.5 13.1 %all_to_all.45 = bf16[8,8,2304]{2,1,0:T(8,128)(2,1)S(1)} all-to-all(bf16[8,8,2304]{2,1,0:T(8,128)(2,1)S(1)} %bitcast.21), channel_id=1, replica_groups={{0,2,4,6,8,10,12,14},{1,3,5,7,9,11,13,15},{16,18,20,22,24,26,28,30},{17..., dimensions={0} | all-to-all | bytes 589824 | tf_op jit(solution)/shard_map/all_to_all | solution.py:528
  46.6 0.0 collective-permute-start
  46.6 1.6 %collective-permute-done.far_ref = bf16[64,2304]{1,0:T(8,128)(2,1)S(1)} collective-permute-done((bf16[64,2304]{1,0:T(8,128)(2,1)S(1)}, bf16[64,2304]{1,0:T(8,128)(2,1)S(1)}, u32[]{:S(2)}, u32[]{:S(2)}) %collective-permute-start) | collective-permute-done | bytes 294944 | tf_op jit(solution)/shard_map/ppermute | solution.py:564
  48.2 12.8 %shard_map.153 = (f32[64,3072]{1,0:T(8,128)S(1)}, f32[64,3072]{1,0:T(8,128)S(1)}) custom-call(bf16[64,2304]{1,0:T(8,128)(2,1)S(1)} %bitcast.15, bf16[64,2304]{1,0:T(8,128)(2,1)S(1)} %collective-permute-done.far_ref, bf16[3072,2048]{1,0:T(8,128)(2,1)} %gate_hbm.1, bf16[3072,2048]{1,0:T(8,128)(2,1)} %up_hbm.1, bf16[2048,3072]{1,0:T(8,128)(2,1)} %down_hbm.1), custom_call_target="tpu_custom_call" | custom-call | flops 4831838208 | bytes 37748736 | tf_op jit(solution)/shard_map/pallas_call | solution.py:81
  61.0 0.2 collective-permute-start.1
  61.2 2.1 %collective-permute-done.1.swapped_ref = f32[64,3072]{1,0:T(8,128)S(1)} collective-permute-done((f32[64,3072]{1,0:T(8,128)S(1)}, f32[64,3072]{1,0:T(8,128)S(1)}, u32[]{:S(2)}, u32[]{:S(2)}) %collective-permute-start.1) | collective-permute-done | bytes 786464 | tf_op jit(solution)/shard_map/ppermute | solution.py:566
  63.4 0.2 shard_map.154
  63.6 13.3 %all_to_all.46 = bf16[8,8,2304]{2,1,0:T(8,128)(2,1)S(1)} all-to-all(bf16[8,8,2304]{2,1,0:T(8,128)(2,1)S(1)} %bitcast.16), channel_id=1, replica_groups={{0,2,4,6,8,10,12,14},{1,3,5,7,9,11,13,15},{16,18,20,22,24,26,28,30},{17..., dimensions={0} | all-to-all | bytes 589824 | tf_op jit(solution)/shard_map/all_to_all | solution.py:528
  76.9 0.8 %shard_map.155 = bf16[8,3072]{1,0:T(8,128)(2,1)} custom-call(bf16[64,2304]{1,0:T(8,128)(2,1)S(1)} %bitcast.17, bf16[16,64]{1,0:T(8,128)(2,1)S(1)} %get-tuple-element.33.main_ref, bf16[3,16,64]{2,1,0:T(8,128)(2,1)S(1)} %get-tuple-element.34.tail_ref, f32[2,8,128]{2,1,0:T(8,128)S(1)} %get-tuple-element.35.gate_ref), custom_call_target="tpu_custom_call" | custom-call | bytes 1048576 | tf_op jit(solution)/shard_map/pallas_call | solution.py:81
Async XLA Ops:
  2.3 16.4 %all-to-all-start = ((bf16[16,8,768]{2,1,0:T(8,128)(2,1)}), bf16[16,8,768]{2,1,0:T(8,128)(2,1)S(1)}, u32[]{:S(2)}, u32[]{:S(2)}) async-start(bf16[16,8,768]{2,1,0:T(8,128)(2,1)} %bitcast.1), calls=%async_computation | async-start | bytes 393216 | tf_op jit(solution)/shard_map/all_to_all | solution.py:528
  46.6 1.6 %collective-permute-start = (bf16[64,2304]{1,0:T(8,128)(2,1)S(1)}, bf16[64,2304]{1,0:T(8,128)(2,1)S(1)}, u32[]{:S(2)}, u32[]{:S(2)}) collective-permute-start(bf16[64,2304]{1,0:T(8,128)(2,1)S(1)} %bitcast.14), channel_id=1, source_target_pairs={{0,1},{1,0},{2,3},{3,2},{4,5},{5,4},{6,7},{7,6},{8,9},{9,8},{10,11... | collective-permute-start | bytes 884744 | tf_op jit(solution)/shard_map/ppermute | solution.py:564
  61.0 2.4 %collective-permute-start.1 = (f32[64,3072]{1,0:T(8,128)S(1)}, f32[64,3072]{1,0:T(8,128)S(1)}, u32[]{:S(2)}, u32[]{:S(2)}) collective-permute-start(f32[64,3072]{1,0:T(8,128)S(1)} %get-tuple-element.32), channel_id=1, source_target_pairs={{0,1},{1,0},{2,3},{3,2},{4,5},{5,4},{6,7},{7,6},{8,9},{9,8},{10,11... | collective-permute-start | bytes 2359304 | tf_op jit(solution)/shard_map/ppermute | solution.py:566

commit v4 on v3

--- a/solution.py
+++ b/solution.py
@@ -1,3 +1,4 @@
+import functools
 import math
 
 import jax
@@ -100,18 +101,19 @@
 
 def send_queries(queries, prefix_of, devices):
     rows = queries.shape[0]
-    holders = devices // PREFIXES
+    chips = devices // 2
+    holders = devices // 2 // PREFIXES
 
     def kernel(query_hbm, prefix_hbm, out_ref, query_ref, prefix_ref, sems):
         copies = fetch([(prefix_hbm, prefix_ref), (query_hbm, query_ref)], sems)
-        row, col = iotas((devices * HK * CAPP, HK * rows))
-        device, k, c = div(row, HK * CAPP), mod(div(row, CAPP), HK), mod(row, CAPP)
+        row, col = iotas((chips * HK * CAPP, HK * rows))
+        chip, k, c = div(row, HK * CAPP), mod(div(row, CAPP), HK), mod(row, CAPP)
         r = mod(col, rows)
         copies[0].wait()
         start = lax.axis_index("wide") * rows
         named, ranks = prefix_slots(prefix_ref, start, rows)
         picked = (
-            (k == div(col, rows)) & (div(device, holders) == by_row(r, named)) & (c == by_row(r, ranks))
+            (k == div(col, rows)) & (div(chip, holders) == by_row(r, named)) & (c == by_row(r, ranks))
         )
         copies[1].wait()
         pieces = stack_pieces(query_ref[...].astype(F32)).astype(BF16)
@@ -119,7 +121,7 @@
 
     return call(
         kernel,
-        jax.ShapeDtypeStruct((devices * HK * CAPP, PIECE), BF16),
+        pltpu.VMEM((chips * HK * CAPP, PIECE), BF16),
         (queries, prefix_of),
         [HBM, HBM],
         scratch=[
@@ -128,6 +130,7 @@
             pltpu.SemaphoreType.DMA((2,)),
         ],
         limit=4,
+        out_specs=VMEM,
     )
 
 
@@ -171,18 +174,26 @@
         stat_ref[own, :] = stat
 
 
-def prefix_block(received, keys, values, devices):
-    total_rows = devices * HK * CAPP
-    slots = devices * CAPP
-
-    def kernel(received_ref, key_ref, value_ref, out_ref):
-        row, col = iotas((total_rows, total_rows))
-        device, slot = mod(div(row, CAPP), devices), mod(row, CAPP)
-        to_heads = (device * (HK * CAPP) + div(row, slots) * CAPP + slot) == col
-        query = dot(one_hot(to_heads), received_ref[...])
+def stats_of(field, head, tops, sums):
+    return by_row(field, [by_row(head, tops), by_row(head, sums)])
+
+
+def prefix_block(near, far, keys, values):
+    side_rows = near.shape[0]
+    total_rows = 2 * side_rows
+    slots = total_rows // HK
+    half = slots // 2
+
+    def kernel(near_ref, far_ref, key_ref, value_ref, kept_ref, given_ref):
+        row, col = iotas((total_rows, side_rows))
+        k, slot = div(row, slots), mod(row, slots)
+        side, slot = div(slot, half), mod(slot, half)
+        source = div(slot, CAPP) * (HK * CAPP) + k * CAPP + mod(slot, CAPP)
+        query = dot(one_hot((side == 0) & (source == col)), near_ref[...]) + dot(
+            one_hot((side == 1) & (source == col)), far_ref[...]
+        )
         lane = iotas((slots, STAT))[1]
         field, head = div(lane, SLOT), mod(lane, SLOT)
-        packed = []
         for k in range(HK):
             cols = pl.ds(k * DH, DH)
             out, top, total = softmax_block(
@@ -191,26 +202,64 @@
                 value_ref[:, cols],
                 None,
             )
-            parts = [out[g * slots : (g + 1) * slots] for g in range(GROUP)]
-            tops = by_row(head, [top[g * slots : (g + 1) * slots] for g in range(GROUP)])
-            sums = by_row(head, [total[g * slots : (g + 1) * slots] for g in range(GROUP)])
-            high = tops.astype(BF16).astype(F32)
-            middle = (tops - high).astype(BF16).astype(F32)
-            low = tops - high - middle
-            sum_high = sums.astype(BF16).astype(F32)
-            stat = by_row(field, [high, middle, low, sum_high, sums - sum_high])
-            packed.append(jnp.concatenate(parts + [stat], axis=1))
-        packed = jnp.concatenate(packed, axis=0).astype(BF16)
-        device, k = div(row, HK * CAPP), mod(div(row, CAPP), HK)
-        to_devices = (k * slots + device * CAPP + slot) == col
-        out_ref[...] = dot(one_hot(to_devices), packed).astype(BF16)
-
-    return call(
-        kernel,
-        jax.ShapeDtypeStruct((total_rows, PIECE + STAT), BF16),
-        (received, keys, values),
-        [VMEM, VMEM, VMEM],
+            tops = [top[g * slots : (g + 1) * slots] for g in range(GROUP)]
+            sums = [total[g * slots : (g + 1) * slots] for g in range(GROUP)]
+            stat = stats_of(field, head, tops, sums)
+            own = pl.ds(k * half, half)
+            for side, ref in enumerate((kept_ref, given_ref)):
+                for g in range(GROUP):
+                    first = g * slots + side * half
+                    ref[own, pl.ds(g * DH, DH)] = out[first : first + half]
+                ref[own, pl.ds(PIECE, STAT)] = stat[side * half : (side + 1) * half]
+
+    part = jax.ShapeDtypeStruct((side_rows, PIECE + STAT), F32)
+    return call(
+        kernel,
+        (part, part),
+        (near, far, keys, values),
+        [VMEM] * 4,
         limit=8,
+    )
+
+
+def join_blocks(kept, swapped):
+    side_rows = kept.shape[0]
+    slots = side_rows // HK
+
+    def kernel(kept_ref, swapped_ref, out_ref):
+        stat = [ref[:, PIECE:] for ref in (kept_ref, swapped_ref)]
+        tops, sums = [s[:, :SLOT] for s in stat], [s[:, SLOT : 2 * SLOT] for s in stat]
+        top = jnp.maximum(*tops)
+        factors = [jnp.exp(t - top) for t in tops]
+        total = factors[0] * sums[0] + factors[1] * sums[1]
+        parts = []
+        for g in range(GROUP):
+            cols = pl.ds(g * DH, DH)
+            parts.append(
+                kept_ref[:, cols] * factors[0][:, g : g + 1]
+                + swapped_ref[:, cols] * factors[1][:, g : g + 1]
+            )
+        lane = iotas((side_rows, STAT))[1]
+        field, head = div(lane, SLOT), mod(lane, SLOT)
+        tops = by_row(head, [top[:, g : g + 1] for g in range(GROUP)])
+        sums = by_row(head, [total[:, g : g + 1] for g in range(GROUP)])
+        high = tops.astype(BF16).astype(F32)
+        middle = (tops - high).astype(BF16).astype(F32)
+        low = tops - high - middle
+        sum_high = sums.astype(BF16).astype(F32)
+        parts.append(by_row(field, [high, middle, low, sum_high, sums - sum_high]))
+        packed = jnp.concatenate(parts, axis=1).astype(BF16)
+        row, col = iotas((side_rows, side_rows))
+        chip, k, c = div(row, HK * CAPP), mod(div(row, CAPP), HK), mod(row, CAPP)
+        out_ref[...] = dot(one_hot(k * slots + chip * CAPP + c == col), packed).astype(BF16)
+
+    return call(
+        kernel,
+        pltpu.VMEM((side_rows, PIECE + STAT), BF16),
+        (kept, swapped),
+        [VMEM, VMEM],
+        limit=4,
+        out_specs=VMEM,
     )
 
 
@@ -258,7 +307,7 @@
 ):
     rows = queries.shape[0]
     half = devices // 2
-    holders = devices // PREFIXES
+    holders = half // PREFIXES
     flat = (rows * suffix_keys.shape[1], suffix_keys.shape[2])
     gain = norm_gain.reshape(1, norm_gain.shape[0])
     expert_index, gate_logits = expert_index.T, gate_logits.T
@@ -288,7 +337,7 @@
 
         named, ranks = prefix_slots(prefix_ref, start, rows)
         firsts = [named[r] * (holders * HK * CAPP) + ranks[r] for r in range(rows)]
-        row, col = iotas((HK * rows, devices * HK * CAPP))
+        row, col = iotas((HK * rows, half * HK * CAPP))
         target = by_row(mod(row, rows), firsts) + div(row, rows) * CAPP
         for h in range(holders):
             find_ref[h] = one_hot(target + h * (HK * CAPP) == col)
@@ -310,7 +359,7 @@
             shape((2 * rows, half * SLOT), BF16),
             shape((BLOCKS, 2 * rows, half * SLOT), BF16),
             shape((2, rows, STAT), F32),
-            shape((holders, HK * rows, devices * HK * CAPP), BF16),
+            shape((holders, HK * rows, half * HK * CAPP), BF16),
             shape(keys.shape, BF16),
             shape(values.shape, BF16),
             shape(hidden_in.shape, BF16),
@@ -457,12 +506,12 @@
             arrive(2 * len(unit_cuts) + n)
             part = dot(hidden_ref[...], down_ref[:, cols])
             mine_ref[:, cols] = part[:half]
-            theirs_ref[:, cols] = part[half:]
-
-    part = jax.ShapeDtypeStruct((half, width), F32)
-    return call(
-        kernel,
-        (part, part),
+            theirs_ref[:, cols] = part[half:].astype(BF16)
+
+    part = functools.partial(jax.ShapeDtypeStruct, (half, width))
+    return call(
+        kernel,
+        (part(F32), part(BF16)),
         (near, far, gate_weight, up_weight, down_weight),
         [VMEM, VMEM, HBM, HBM, HBM],
         flops=12 * half * units * width,
@@ -488,11 +537,11 @@
         i, i_from = mod(row, SLOT), mod(col, SLOT)
         keep = mod(iotas((half, PIECE))[0], SLOT) < CAPE
         last = pl.ds(BLOCKS * PIECE, PIECE)
-        tail = (mine_ref[:, last] + swapped_ref[:, last]).astype(BF16)
+        tail = (mine_ref[:, last] + swapped_ref[:, last].astype(F32)).astype(BF16)
         for n in range(BLOCKS):
             cols = pl.ds(n * PIECE, PIECE)
             moved = dot(one_hot(same & (i >= CAPE) & (i_from == (i - CAPE) * PER + n)), tail)
-            out_ref[:, cols] = jnp.where(keep, mine_ref[:, cols] + swapped_ref[:, cols], moved).astype(BF16)
+            out_ref[:, cols] = jnp.where(keep, mine_ref[:, cols] + swapped_ref[:, cols].astype(F32), moved).astype(BF16)
 
     return call(
         kernel,
@@ -524,7 +573,7 @@
     )
 
 
-def exchange(x, groups=None):
+def exchange(x, groups):
     return lax.all_to_all(x, "wide", 0, 0, tiled=True, axis_index_groups=groups)
 
 
@@ -553,12 +602,16 @@
 
     outgoing = send_queries(queries, prefix_of, devices)
     outgoing, suffix_length = lax.optimization_barrier((outgoing, suffix_length))
-    received = exchange(outgoing)
+    near = exchange(outgoing, alike)
     suffix_out, suffix_stat, pack, main, tail, gates, find, keys, values, hidden, gain = prepare(
         queries, suffix_keys, suffix_values, suffix_length, prefix_of, expert_index, gate_logits,
         prefix_keys, prefix_values, hidden_in, norm_gain, devices,
     )
-    back = exchange(prefix_block(received, keys, values, devices))
+    near, keys = lax.optimization_barrier((near, keys))
+    far = lax.ppermute(near, "wide", siblings)
+    kept, given = prefix_block(near, far, keys, values)
+    swapped = lax.ppermute(given, "wide", siblings)
+    back = exchange(join_blocks(kept, swapped), alike)
     attended, sent = merge(back, suffix_out, suffix_stat, hidden, gain, find, pack, devices)
     near = exchange(sent, alike)
     far = lax.ppermute(near, "wide", siblings)

time: 78.1 us -> 76 us (0.973)
  blocking collectives: 38.5 us -> 35.7 us
    all_to_all x3, blocking collectives: 38.5 us -> 35.7 us  [exchange(): return lax.all_to_all(x, 'wide', 0, 0, tiled=True, axis_index_groups=groups)]
    all_to_all x1, waiting for transfers between devices: 6.48 us -> 4.66 us  [exchange(): return lax.all_to_all(x, 'wide', 0, 0, tiled=True, axis_index_groups=groups)]
    ppermute x0 -> x1, waiting for transfers between devices: none -> 1.34 us  [local(): swapped = lax.ppermute(given, 'wide', siblings)]
    ppermute x1 -> x2, waiting for transfers between devices: 1.58 us -> 2.88 us  [local(): far = lax.ppermute(near, 'wide', siblings)]
    pallas_call x7 -> x8, Pallas kernels: 20.7 us -> 21 us  [call(): pl.pallas_call(kernel, out_shape=outs, in_specs=specs, out_specs=out_spec...]
  transfers between devices with their start and end apart: 3 -> 5, of which waited for: 3 -> 5; matrix products, arithmetic and copies ran while one was open for 0% -> 0% of each run, Pallas kernels for 3% -> 3%
where the time goes in v4:
time: 76 us; the launch traced here: 75.6 us
  blocking collectives  35.7 us (47%)
  Pallas kernels  21 us (28%)
  waiting for transfers between devices  10.5 us (14%)
  starting transfers between devices  7.74 us (10%)
    all_to_all x3, blocking collectives, exchange(): return lax.all_to_all(x, 'wide', 0, 0, tiled=True, axis_index_groups=groups)  35.7 us
    pallas_call x8, Pallas kernels, call(): pl.pallas_call(kernel, out_shape=outs, in_specs=specs, out_specs=out_spec...  21 us
    all_to_all x1, starting transfers between devices, exchange(): return lax.all_to_all(x, 'wide', 0, 0, tiled=True, axis_index_groups=groups)  7.32 us
    all_to_all x1, waiting for transfers between devices, exchange(): return lax.all_to_all(x, 'wide', 0, 0, tiled=True, axis_index_groups=groups)  4.66 us
    ppermute x2, waiting for transfers between devices, local(): far = lax.ppermute(near, 'wide', siblings)  2.88 us
    ppermute x1, waiting for transfers between devices, local(): swapped = lax.ppermute(theirs, 'wide', siblings)  1.59 us
  transfers between devices with their start and end apart: 5, of which 5 were waited for; matrix products, arithmetic and copies ran while one was open for 0% of the time, Pallas kernels for 3%

profile of v4, /device:TPU:0, one launch (start us, length us, event | category | flops | bytes accessed | tf_op | source)
XLA Modules:
  0.0 75.6 jit_solution(2811562222768861435)
XLA Ops:
  0.6 1.6 %shard_map.149 = bf16[64,768]{1,0:T(8,128)(2,1)} custom-call(bf16[8,3072]{1,0:T(8,128)(2,1)} %query_hbm.3, s32[128]{0:T(128)} %bitcast.23), custom_call_target="tpu_custom_call" | custom-call | bytes 1048576 | tf_op jit(solution)/shard_map/pallas_call | solution.py:82
  2.2 7.3 %all-to-all-start = ((bf16[8,8,768]{2,1,0:T(8,128)(2,1)}), bf16[8,8,768]{2,1,0:T(8,128)(2,1)S(1)}, u32[]{:S(2)}, u32[]{:S(2)}) async-start(bf16[8,8,768]{2,1,0:T(8,128)(2,1)} %bitcast.1), calls=%async_computation | async-start | bytes 196608 | tf_op jit(solution)/shard_map/all_to_all | solution.py:577
  9.6 2.5 %shard_map.150 = (f32[32,768]{1,0:T(8,128)S(1)}, f32[32,128]{1,0:T(8,128)S(1)}, bf16[3,32,32]{2,1,0:T(8,128)(2,1)S(1)}, bf16[16,64]{1,0:T(8,128)(2,1)S(1)}, bf16...) custom-call(bf16[8,3072]{1,0:T(8,128)(2,1)} %query_hbm.3, ...), custom_call_target="tpu_custom_call" | custom-call | flops 2147483648 | bytes 1048576 | tf_op jit(solution)/shard_map/pallas_call | solution.py:82
  12.0 4.7 %all-to-all-done = bf16[8,8,768]{2,1,0:T(8,128)(2,1)S(1)} async-done(((bf16[8,8,768]{2,1,0:T(8,128)(2,1)}), bf16[8,8,768]{2,1,0:T(8,128)(2,1)S(1)}, u32[]{:S(2)}, u32[]{:S(2)}) %all-to-all-start) | async-done | bytes 98336 | tf_op jit(solution)/shard_map/all_to_all | solution.py:577
  16.7 0.0 collective-permute-start
  16.7 1.3 %collective-permute-done.far_ref = bf16[64,768]{1,0:T(8,128)(2,1)S(1)} collective-permute-done((bf16[64,768]{1,0:T(8,128)(2,1)S(1)}, bf16[64,768]{1,0:T(8,128)(2,1)S(1)}, u32[]{:S(2)}, u32[]{:S(2)}) %collective-permute-start) | collective-permute-done | bytes 98336 | tf_op jit(solution)/shard_map/ppermute | solution.py:611
  18.0 1.5 %shard_map.151 = (f32[64,896]{1,0:T(8,128)S(1)}, f32[64,896]{1,0:T(8,128)S(1)}) custom-call(bf16[64,768]{1,0:T(8,128)(2,1)S(1)} %bitcast.21, bf16[64,768]{1,0:T(8,128)(2,1)S(1)} %collective-permute-done.far_ref, bf16[512,512]{1,0:T(8,128)(2,1)S(1)} %get-tuple-element.27.key_ref, bf16[512,512]{1,0:T(8,128)(2,1)S(1)} %get-tuple-element.28.value_ref), custom_call_target="tpu_custom_call" | custom-call | bytes 1048576 | tf_op jit(solution)/shard_map/pallas_call | solution.py:82
  19.5 0.2 collective-permute-start.1
  19.8 1.3 %collective-permute-done.1.swapped_ref = f32[64,896]{1,0:T(8,128)S(1)} collective-permute-done((f32[64,896]{1,0:T(8,128)S(1)}, f32[64,896]{1,0:T(8,128)S(1)}, u32[]{:S(2)}, u32[]{:S(2)}) %collective-permute-start.1) | collective-permute-done | bytes 229408 | tf_op jit(solution)/shard_map/ppermute | solution.py:613
  21.1 0.5 shard_map.152
  21.6 9.7 %all_to_all.45 = bf16[8,8,896]{2,1,0:T(8,128)(2,1)S(1)} all-to-all(bf16[8,8,896]{2,1,0:T(8,128)(2,1)S(1)} %bitcast.19), channel_id=1, replica_groups={{0,2,4,6,8,10,12,14},{1,3,5,7,9,11,13,15},{16,18,20,22,24,26,28,30},{17..., dimensions={0} | all-to-all | bytes 229376 | tf_op jit(solution)/shard_map/all_to_all | solution.py:577
  31.3 1.0 %shard_map.153 = (bf16[8,3072]{1,0:T(8,128)(2,1)}, bf16[64,2304]{1,0:T(8,128)(2,1)S(1)}) custom-call(bf16[64,896]{1,0:T(8,128)(2,1)S(1)} %bitcast.18, f32[32,768]{1,0:T(8,128)S(1)} %get-tuple-element.31.suffix_ref, f32[32,128]{1,0:T(8,128)S(1)} %get-tuple-element.32.stat_ref, bf16[8,3072]{1,0:T(8,128)(2,1)S(1)} %get-tuple-element.33.hidden_ref, ...), custom_call_target="tpu_custom_call" | custom-call | bytes 1048576 | tf_op jit(solution)/shard_map/pallas_call | solution.py:82
  32.3 12.7 %all_to_all.46 = bf16[8,8,2304]{2,1,0:T(8,128)(2,1)S(1)} all-to-all(bf16[8,8,2304]{2,1,0:T(8,128)(2,1)S(1)} %bitcast.22), channel_id=1, replica_groups={{0,2,4,6,8,10,12,14},{1,3,5,7,9,11,13,15},{16,18,20,22,24,26,28,30},{17..., dimensions={0} | all-to-all | bytes 589824 | tf_op jit(solution)/shard_map/all_to_all | solution.py:577
  45.0 0.0 collective-permute-start.2
  45.0 1.6 %collective-permute-done.2.far_ref = bf16[64,2304]{1,0:T(8,128)(2,1)S(1)} collective-permute-done((bf16[64,2304]{1,0:T(8,128)(2,1)S(1)}, bf16[64,2304]{1,0:T(8,128)(2,1)S(1)}, u32[]{:S(2)}, u32[]{:S(2)}) %collective-permute-start.2) | collective-permute-done | bytes 294944 | tf_op jit(solution)/shard_map/ppermute | solution.py:617
  46.6 12.8 %shard_map.154 = (f32[64,3072]{1,0:T(8,128)S(1)}, bf16[64,3072]{1,0:T(8,128)(2,1)S(1)}) custom-call(bf16[64,2304]{1,0:T(8,128)(2,1)S(1)} %bitcast.15, bf16[64,2304]{1,0:T(8,128)(2,1)S(1)} %collective-permute-done.2.far_ref, bf16[3072,2048]{1,0:T(8,128)(2,1)} %gate_hbm.1, bf16[3072,2048]{1,0:T(8,128)(2,1)} %up_hbm.1, bf16[2048,3072]{1,0:T(8,128)(2,1)} %down_hbm.1), custom_call_target="tpu_custom_call" | custom-call | flops 4831838208 | bytes 37748736 | tf_op jit(solution)/shard_map/pallas_call | solution.py:82
  59.4 0.2 collective-permute-start.3
  59.6 1.6 %collective-permute-done.3.swapped_ref = bf16[64,3072]{1,0:T(8,128)(2,1)S(1)} collective-permute-done((bf16[64,3072]{1,0:T(8,128)(2,1)S(1)}, bf16[64,3072]{1,0:T(8,128)(2,1)S(1)}, u32[]{:S(2)}, u32[]{:S(2)}) %collective-permute-start.3) | collective-permute-done | bytes 393248 | tf_op jit(solution)/shard_map/ppermute | solution.py:619
  61.2 0.2 shard_map.155
  61.4 13.3 %all_to_all.47 = bf16[8,8,2304]{2,1,0:T(8,128)(2,1)S(1)} all-to-all(bf16[8,8,2304]{2,1,0:T(8,128)(2,1)S(1)} %bitcast.17), channel_id=1, replica_groups={{0,2,4,6,8,10,12,14},{1,3,5,7,9,11,13,15},{16,18,20,22,24,26,28,30},{17..., dimensions={0} | all-to-all | bytes 589824 | tf_op jit(solution)/shard_map/all_to_all | solution.py:577
  74.8 0.8 %shard_map.156 = bf16[8,3072]{1,0:T(8,128)(2,1)} custom-call(bf16[64,2304]{1,0:T(8,128)(2,1)S(1)} %bitcast.16, bf16[16,64]{1,0:T(8,128)(2,1)S(1)} %get-tuple-element.41.main_ref, bf16[3,16,64]{2,1,0:T(8,128)(2,1)S(1)} %get-tuple-element.42.tail_ref, f32[2,8,128]{2,1,0:T(8,128)S(1)} %get-tuple-element.43.gate_ref), custom_call_target="tpu_custom_call" | custom-call | bytes 1048576 | tf_op jit(solution)/shard_map/pallas_call | solution.py:82
Async XLA Ops:
  2.2 14.4 %all-to-all-start = ((bf16[8,8,768]{2,1,0:T(8,128)(2,1)}), bf16[8,8,768]{2,1,0:T(8,128)(2,1)S(1)}, u32[]{:S(2)}, u32[]{:S(2)}) async-start(bf16[8,8,768]{2,1,0:T(8,128)(2,1)} %bitcast.1), calls=%async_computation | async-start | bytes 196608 | tf_op jit(solution)/shard_map/all_to_all | solution.py:577
  16.7 1.3 %collective-permute-start = (bf16[64,768]{1,0:T(8,128)(2,1)S(1)}, bf16[64,768]{1,0:T(8,128)(2,1)S(1)}, u32[]{:S(2)}, u32[]{:S(2)}) collective-permute-start(bf16[64,768]{1,0:T(8,128)(2,1)S(1)} %bitcast.20), channel_id=1, source_target_pairs={{0,1},{1,0},{2,3},{3,2},{4,5},{5,4},{6,7},{7,6},{8,9},{9,8},{10,11... | collective-permute-start | bytes 294920 | tf_op jit(solution)/shard_map/ppermute | solution.py:611
  19.5 1.6 %collective-permute-start.1 = (f32[64,896]{1,0:T(8,128)S(1)}, f32[64,896]{1,0:T(8,128)S(1)}, u32[]{:S(2)}, u32[]{:S(2)}) collective-permute-start(f32[64,896]{1,0:T(8,128)S(1)} %get-tuple-element.30), channel_id=1, source_target_pairs={{0,1},{1,0},{2,3},{3,2},{4,5},{5,4},{6,7},{7,6},{8,9},{9,8},{10,11... | collective-permute-start | bytes 688136 | tf_op jit(solution)/shard_map/ppermute | solution.py:613
  45.0 1.6 %collective-permute-start.2 = (bf16[64,2304]{1,0:T(8,128)(2,1)S(1)}, bf16[64,2304]{1,0:T(8,128)(2,1)S(1)}, u32[]{:S(2)}, u32[]{:S(2)}) collective-permute-start(bf16[64,2304]{1,0:T(8,128)(2,1)S(1)} %bitcast.14), channel_id=1, source_target_pairs={{0,1},{1,0},{2,3},{3,2},{4,5},{5,4},{6,7},{7,6},{8,9},{9,8},{10,11... | collective-permute-start | bytes 884744 | tf_op jit(solution)/shard_map/ppermute | solution.py:617
  59.4 1.8 %collective-permute-start.3 = (bf16[64,3072]{1,0:T(8,128)(2,1)S(1)}, bf16[64,3072]{1,0:T(8,128)(2,1)S(1)}, u32[]{:S(2)}, u32[]{:S(2)}) collective-permute-start(bf16[64,3072]{1,0:T(8,128)(2,1)S(1)} %get-tuple-element.40), channel_id=1, source_target_pairs={{0,1},{1,0},{2,3},{3,2},{4,5},{5,4},{6,7},{7,6},{8,9},{9,8},{10,11... | collective-permute-start | bytes 1179656 | tf_op jit(solution)/shard_map/ppermute | solution.py:619

commit v5 on v4

--- a/solution.py
+++ b/solution.py
@@ -148,13 +148,9 @@
     return jnp.concatenate([x[:, g * DH : (g + 1) * DH] for g in range(GROUP)], axis=0)
 
 
-def own_suffix(query, key_ref, value_ref, lengths, out_ref, stat_ref):
+def own_suffix(query, key_ref, value_ref, live, out_ref, stat_ref):
     rows = query.shape[0]
-    span = key_ref.shape[0] // rows
-    row, col = iotas((rows, rows * span))
-    owner = div(col, span)
-    live = (owner == row) & (mod(col, span) < by_row(owner, lengths))
-    mask = jnp.concatenate([live.astype(F32)] * GROUP, axis=0) > 0.5
+    mask = jnp.concatenate([live] * GROUP, axis=0) > 0.5
     lane = iotas((rows, STAT))[1]
     for k in range(HK):
         cols = pl.ds(k * DH, DH)
@@ -263,9 +259,8 @@
     )
 
 
-def routes(named, logits, half, pack_ref, main_ref, tail_ref, gate_ref):
+def routes_out(named, pack_ref):
     rows = len(named[0])
-    per_expert = half // EXPERTS
     row, col = iotas((EXPERTS * SLOT, HK * rows))
     expert, i, k, r = div(row, SLOT), mod(row, SLOT), div(col, rows), mod(col, rows)
     has = (by_row(r, named[0]) == expert) | (by_row(r, named[1]) == expert)
@@ -277,6 +272,10 @@
         piece = jnp.where(i < CAPE, n, HK - 1)
         pack_ref[n] = one_hot(has & (rank == slot) & (k == piece))
 
+
+def routes_back(named, logits, half, main_ref, tail_ref, gate_ref):
+    rows = len(named[0])
+    per_expert = half // EXPERTS
     row, col = iotas((2 * rows, half * SLOT))
     j, r = div(row, rows), mod(row, rows)
     expert, i = div(div(col, SLOT), per_expert), mod(col, SLOT)
@@ -301,87 +300,123 @@
     gate_ref[1] = second / (first + second)
 
 
-def prepare(
-    queries, suffix_keys, suffix_values, lengths, prefix_of, expert_index, gate_logits,
-    keys, values, hidden_in, norm_gain, devices,
-):
-    rows = queries.shape[0]
+def own_experts(expert_ref, start, rows):
+    return [[expert_ref[j, start + r] for r in range(rows)] for j in range(2)]
+
+
+def stage(prefix_of, expert_index, lengths, arrays, after, devices, rows, span):
     half = devices // 2
     holders = half // PREFIXES
-    flat = (rows * suffix_keys.shape[1], suffix_keys.shape[2])
-    gain = norm_gain.reshape(1, norm_gain.shape[0])
-    expert_index, gate_logits = expert_index.T, gate_logits.T
-
-    def kernel(
-        query_hbm, skey_hbm, svalue_hbm, length_hbm, prefix_hbm, expert_hbm, logit_hbm,
-        key_hbm, value_hbm, hidden_hbm, gain_hbm,
-        suffix_ref, stat_ref, pack_ref, main_ref, tail_ref, gate_ref, find_ref,
-        key_ref, value_ref, hidden_ref, gain_ref,
-        query_ref, skey_ref, svalue_ref, length_ref, prefix_ref, expert_ref, logit_ref, sems,
-    ):
+    expert_index = expert_index.T
+    count = len(arrays)
+
+    def kernel(*refs):
+        _, prefix_hbm, expert_hbm, length_hbm = refs[:4]
+        sources, outs = refs[4 : 4 + count], refs[4 + count : 4 + 2 * count]
+        find_ref, pack_ref, live_ref, prefix_ref, expert_ref, length_ref, sems = refs[4 + 2 * count :]
         copies = fetch(
             [
-                (expert_hbm, expert_ref), (logit_hbm, logit_ref), (prefix_hbm, prefix_ref),
-                (length_hbm, length_ref), (query_hbm, query_ref), (skey_hbm, skey_ref),
-                (svalue_hbm, svalue_ref), (key_hbm, key_ref), (value_hbm, value_ref),
-                (hidden_hbm, hidden_ref), (gain_hbm, gain_ref),
+                (prefix_hbm, prefix_ref), (expert_hbm, expert_ref), (length_hbm, length_ref),
+                *zip(sources, outs),
             ],
             sems,
         )
         start = lax.axis_index("wide") * rows
         for copy in copies[:3]:
             copy.wait()
-        named = [[expert_ref[j, start + r] for r in range(rows)] for j in range(2)]
-        logits = [[logit_ref[j, start + r] for r in range(rows)] for j in range(2)]
-        routes(named, logits, half, pack_ref, main_ref, tail_ref, gate_ref)
-
+        row, col = iotas((rows, rows * span))
+        owner = div(col, span)
+        length = by_row(owner, [length_ref[r] for r in range(rows)])
+        live_ref[...] = ((owner == row) & (mod(col, span) < length)).astype(F32)
         named, ranks = prefix_slots(prefix_ref, start, rows)
         firsts = [named[r] * (holders * HK * CAPP) + ranks[r] for r in range(rows)]
         row, col = iotas((HK * rows, half * HK * CAPP))
         target = by_row(mod(row, rows), firsts) + div(row, rows) * CAPP
         for h in range(holders):
             find_ref[h] = one_hot(target + h * (HK * CAPP) == col)
-
-        for copy in copies[3:7]:
+        routes_out(own_experts(expert_ref, start, rows), pack_ref)
+        for copy in copies[3:]:
             copy.wait()
-        lengths = [length_ref[r] for r in range(rows)]
-        own_suffix(query_ref[...].astype(F32), skey_ref, svalue_ref, lengths, suffix_ref, stat_ref)
-        for copy in copies[7:]:
-            copy.wait()
-
-    shape = jax.ShapeDtypeStruct
+
     return call(
         kernel,
         (
-            shape((HK * rows, PIECE), F32),
-            shape((HK * rows, STAT), F32),
-            shape((BLOCKS, EXPERTS * SLOT, HK * rows), BF16),
-            shape((2 * rows, half * SLOT), BF16),
-            shape((BLOCKS, 2 * rows, half * SLOT), BF16),
-            shape((2, rows, STAT), F32),
-            shape((holders, HK * rows, half * HK * CAPP), BF16),
-            shape(keys.shape, BF16),
-            shape(values.shape, BF16),
-            shape(hidden_in.shape, BF16),
-            shape(gain.shape, F32),
+            *[pltpu.VMEM(x.shape, x.dtype) for x in arrays],
+            pltpu.VMEM((holders, HK * rows, half * HK * CAPP), BF16),
+            pltpu.VMEM((BLOCKS, EXPERTS * SLOT, HK * rows), BF16),
+            pltpu.VMEM((rows, rows * span), F32),
         ),
-        (
-            queries, suffix_keys.reshape(flat), suffix_values.reshape(flat), lengths, prefix_of,
-            expert_index, gate_logits, keys, values, hidden_in, gain,
-        ),
-        [HBM] * 11,
-        flops=1 << 31,
+        (after, prefix_of, expert_index, lengths, *arrays),
+        [VMEM] + [HBM] * (3 + count),
+        flops=1 << 30,
         scratch=[
-            pltpu.VMEM(queries.shape, BF16),
-            pltpu.VMEM(flat, BF16),
-            pltpu.VMEM(flat, BF16),
-            pltpu.SMEM(lengths.shape, jnp.int32),
             pltpu.SMEM(prefix_of.shape, jnp.int32),
             pltpu.SMEM(expert_index.shape, jnp.int32),
+            pltpu.SMEM(lengths.shape, jnp.int32),
+            pltpu.SemaphoreType.DMA((3 + count,)),
+        ],
+        out_specs=(VMEM,) * (3 + count),
+        limit=4,
+    )
+
+
+def suffix_block(queries, keys, values, live, after):
+    rows = queries.shape[0]
+
+    def kernel(_, query_ref, key_ref, value_ref, live_ref, out_ref, stat_ref):
+        own_suffix(
+            query_ref[...].astype(F32), key_ref, value_ref, live_ref[...], out_ref, stat_ref
+        )
+
+    return call(
+        kernel,
+        (pltpu.VMEM((HK * rows, PIECE), F32), pltpu.VMEM((HK * rows, STAT), F32)),
+        (after, queries, keys, values, live),
+        [VMEM] * 5,
+        flops=1 << 30,
+        out_specs=(VMEM, VMEM),
+        limit=4,
+    )
+
+
+def finish(attended, expert_index, gate_logits, after, devices):
+    rows = attended.shape[0]
+    half = devices // 2
+    expert_index, gate_logits = expert_index.T, gate_logits.T
+
+    def kernel(
+        _, attended_ref, expert_hbm, logit_hbm,
+        out_hbm, main_ref, tail_ref, gate_ref, expert_ref, logit_ref, sems,
+    ):
+        copies = fetch(
+            [(expert_hbm, expert_ref), (logit_hbm, logit_ref), (attended_ref, out_hbm)], sems
+        )
+        start = lax.axis_index("wide") * rows
+        for copy in copies[:2]:
+            copy.wait()
+        named = own_experts(expert_ref, start, rows)
+        logits = own_experts(logit_ref, start, rows)
+        routes_back(named, logits, half, main_ref, tail_ref, gate_ref)
+        copies[2].wait()
+
+    return call(
+        kernel,
+        (
+            pltpu.HBM(attended.shape, attended.dtype),
+            pltpu.VMEM((2 * rows, half * SLOT), BF16),
+            pltpu.VMEM((BLOCKS, 2 * rows, half * SLOT), BF16),
+            pltpu.VMEM((2, rows, STAT), F32),
+        ),
+        (after, attended, expert_index, gate_logits),
+        [VMEM, VMEM, HBM, HBM],
+        flops=1 << 30,
+        scratch=[
+            pltpu.SMEM(expert_index.shape, jnp.int32),
             pltpu.SMEM(gate_logits.shape, F32),
-            pltpu.SemaphoreType.DMA((11,)),
+            pltpu.SemaphoreType.DMA((3,)),
         ],
-        limit=8,
+        out_specs=(HBM, VMEM, VMEM, VMEM),
+        limit=4,
     )
 
 
@@ -438,12 +473,13 @@
     return call(
         kernel,
         (
-            jax.ShapeDtypeStruct((rows, width), BF16),
-            jax.ShapeDtypeStruct((half * SLOT, BLOCKS * PIECE), BF16),
+            pltpu.VMEM((rows, width), BF16),
+            pltpu.VMEM((half * SLOT, BLOCKS * PIECE), BF16),
         ),
         (back, suffix_out, suffix_stat, hidden_in, gain, find, pack),
         [VMEM] * 7,
         limit=8,
+        out_specs=(VMEM, VMEM),
     )
 
 
@@ -601,20 +637,32 @@
     prefix_of = prefix_of[:, 0]
 
     outgoing = send_queries(queries, prefix_of, devices)
-    outgoing, suffix_length = lax.optimization_barrier((outgoing, suffix_length))
     near = exchange(outgoing, alike)
-    suffix_out, suffix_stat, pack, main, tail, gates, find, keys, values, hidden, gain = prepare(
-        queries, suffix_keys, suffix_values, suffix_length, prefix_of, expert_index, gate_logits,
-        prefix_keys, prefix_values, hidden_in, norm_gain, devices,
-    )
-    near, keys = lax.optimization_barrier((near, keys))
     far = lax.ppermute(near, "wide", siblings)
+    flat = (-1, suffix_keys.shape[2])
+    keys, values, suffix_keys, suffix_values, own, hidden, gain, find, pack, live = stage(
+        prefix_of,
+        expert_index,
+        suffix_length,
+        (
+            prefix_keys, prefix_values, suffix_keys.reshape(flat), suffix_values.reshape(flat),
+            queries, hidden_in, norm_gain.reshape(1, -1),
+        ),
+        near,
+        devices,
+        rows,
+        suffix_keys.shape[1],
+    )
     kept, given = prefix_block(near, far, keys, values)
     swapped = lax.ppermute(given, "wide", siblings)
+    suffix_out, suffix_stat = suffix_block(own, suffix_keys, suffix_values, live, kept)
+    swapped, suffix_stat = lax.optimization_barrier((swapped, suffix_stat))
     back = exchange(join_blocks(kept, swapped), alike)
     attended, sent = merge(back, suffix_out, suffix_stat, hidden, gain, find, pack, devices)
     near = exchange(sent, alike)
     far = lax.ppermute(near, "wide", siblings)
+    attended, main, tail, gates = finish(attended, expert_index, gate_logits, near, devices)
+    far, gates = lax.optimization_barrier((far, gates))
     mine, theirs = experts(near, far, gate_weight, up_weight, down_weight)
     swapped = lax.ppermute(theirs, "wide", siblings)
     parts = exchange(add_and_pack(mine, swapped), alike)

time: 76 us -> 75.5 us (level)
  blocking collectives: 35.7 us -> 50.2 us
  waiting for transfers between devices: 10.5 us -> 2.37 us
  starting transfers between devices: 7.74 us -> 0.78 us
    all_to_all x3 -> x4, blocking collectives: 35.7 us -> 50.2 us  [exchange(): return lax.all_to_all(x, 'wide', 0, 0, tiled=True, axis_index_groups=groups)]
    all_to_all x1 -> x0, starting transfers between devices: 7.32 us -> none  [exchange(): return lax.all_to_all(x, 'wide', 0, 0, tiled=True, axis_index_groups=groups)]
    all_to_all x1 -> x0, waiting for transfers between devices: 4.66 us -> none  [exchange(): return lax.all_to_all(x, 'wide', 0, 0, tiled=True, axis_index_groups=groups)]
    ppermute x2, waiting for transfers between devices: 2.88 us -> 0.78 us  [local(): far = lax.ppermute(near, 'wide', siblings)]
    ppermute x1, waiting for transfers between devices: 1.34 us -> 0.01 us  [local(): swapped = lax.ppermute(given, 'wide', siblings)]
    pallas_call x8 -> x10, Pallas kernels: 21 us -> 21.1 us  [call(): pl.pallas_call(kernel, out_shape=outs, in_specs=specs, out_specs=out_spec...]
  transfers between devices with their start and end apart: 5 -> 4, of which waited for: 5 -> 2; matrix products, arithmetic and copies ran while one was open for 0% -> 0% of each run, Pallas kernels for 3% -> 5%
where the time goes in v5:
time: 75.5 us; the launch traced here: 75.1 us
  blocking collectives  50.2 us (66%)
  Pallas kernels  21.1 us (28%)
  waiting for transfers between devices  2.37 us (3%)
  starting transfers between devices  0.78 us (1%)
    all_to_all x4, blocking collectives, exchange(): return lax.all_to_all(x, 'wide', 0, 0, tiled=True, axis_index_groups=groups)  50.2 us
    pallas_call x10, Pallas kernels, call(): pl.pallas_call(kernel, out_shape=outs, in_specs=specs, out_specs=out_spec...  21.1 us
    ppermute x1, waiting for transfers between devices, local(): swapped = lax.ppermute(theirs, 'wide', siblings)  1.59 us
  transfers between devices with their start and end apart: 4, of which 2 were waited for; matrix products, arithmetic and copies ran while one was open for 0% of the time, Pallas kernels for 5%

profile of v5, /device:TPU:0, one launch (start us, length us, event | category | flops | bytes accessed | tf_op | source)
XLA Modules:
  0.0 75.1 jit_solution(1630346815907254006)
XLA Ops:
  0.6 1.0 %shard_map.149 = bf16[64,768]{1,0:T(8,128)(2,1)S(1)} custom-call(bf16[8,3072]{1,0:T(8,128)(2,1)} %refs_8_.1, s32[128]{0:T(128)} %bitcast.26), custom_call_target="tpu_custom_call" | custom-call | bytes 1048576 | tf_op jit(solution)/shard_map/pallas_call | solution.py:82
  1.6 14.2 %all_to_all.44 = bf16[8,8,768]{2,1,0:T(8,128)(2,1)S(1)} all-to-all(bf16[8,8,768]{2,1,0:T(8,128)(2,1)S(1)} %bitcast.24), channel_id=1, replica_groups={{0,2,4,6,8,10,12,14},{1,3,5,7,9,11,13,15},{16,18,20,22,24,26,28,30},{17..., dimensions={0} | all-to-all | bytes 196608 | tf_op jit(solution)/shard_map/all_to_all | solution.py:613
  15.8 0.0 collective-permute-start
  15.8 1.6 %shard_map.150 = (bf16[512,512]{1,0:T(8,128)(2,1)S(1)}, bf16[512,512]{1,0:T(8,128)(2,1)S(1)}, bf16[512,512]{1,0:T(8,128)(2,1)S(1)}, bf16[512,512]{1,0:T(8,128)(2...) custom-call(bf16[64,768]{1,0:T(8,128)(2,1)S(1)} %bitcast.22, ...), custom_call_target="tpu_custom_call" | custom-call | flops 1073741824 | bytes 1048576 | tf_op jit(solution)/shard_map/pallas_call | solution.py:82
  17.5 0.0 collective-permute-done.far_ref
  17.5 1.5 %shard_map.151 = (f32[64,896]{1,0:T(8,128)S(1)}, f32[64,896]{1,0:T(8,128)S(1)}) custom-call(bf16[64,768]{1,0:T(8,128)(2,1)S(1)} %bitcast.23, bf16[64,768]{1,0:T(8,128)(2,1)S(1)} %collective-permute-done.far_ref, bf16[512,512]{1,0:T(8,128)(2,1)S(1)} %get-tuple-element.28.key_ref, bf16[512,512]{1,0:T(8,128)(2,1)S(1)} %get-tuple-element.29.value_ref), custom_call_target="tpu_custom_call" | custom-call | bytes 1048576 | tf_op jit(solution)/shard_map/pallas_call | solution.py:82
  19.0 0.6 collective-permute-start.1
  19.6 1.1 %shard_map.152 = (f32[32,768]{1,0:T(8,128)S(1)}, f32[32,128]{1,0:T(8,128)S(1)}) custom-call(f32[64,896]{1,0:T(8,128)S(1)} %get-tuple-element.30._.kept_ref, bf16[8,3072]{1,0:T(8,128)(2,1)S(1)} %get-tuple-element.32.query_ref, bf16[512,512]{1,0:T(8,128)(2,1)S(1)} %get-tuple-element.33.key_ref, bf16[512,512]{1,0:T(8,128)(2,1)S(1)} %get-tuple-element.34.value_ref, ...), custom_call_target="tpu_custom_call" | custom-call | flops 1073741824 | bytes 1048576 | tf_op jit(solution)/shard_map/pallas_call | solution.py:82
  20.7 0.0 collective-permute-done.1.swapped_ref
  20.7 0.5 shard_map.153
  21.2 9.9 %all_to_all.45 = bf16[8,8,896]{2,1,0:T(8,128)(2,1)S(1)} all-to-all(bf16[8,8,896]{2,1,0:T(8,128)(2,1)S(1)} %bitcast.20), channel_id=1, replica_groups={{0,2,4,6,8,10,12,14},{1,3,5,7,9,11,13,15},{16,18,20,22,24,26,28,30},{17..., dimensions={0} | all-to-all | bytes 229376 | tf_op jit(solution)/shard_map/all_to_all | solution.py:613
  31.1 0.7 shard_map.154
  31.9 12.7 %all_to_all.46 = bf16[8,8,2304]{2,1,0:T(8,128)(2,1)S(1)} all-to-all(bf16[8,8,2304]{2,1,0:T(8,128)(2,1)S(1)} %bitcast.25), channel_id=1, replica_groups={{0,2,4,6,8,10,12,14},{1,3,5,7,9,11,13,15},{16,18,20,22,24,26,28,30},{17..., dimensions={0} | all-to-all | bytes 589824 | tf_op jit(solution)/shard_map/all_to_all | solution.py:613
  44.6 0.0 collective-permute-start.2
  44.6 0.8 %shard_map.155 = (bf16[8,3072]{1,0:T(8,128)(2,1)}, bf16[16,64]{1,0:T(8,128)(2,1)S(1)}, bf16[3,16,64]{2,1,0:T(8,128)(2,1)S(1)}, f32[2,8,128]{2,1,0:T(8,128)S(1)}) custom-call(bf16[64,2304]{1,0:T(8,128)(2,1)S(1)} %bitcast.15, bf16[8,3072]{1,0:T(8,128)(2,1)S(1)} %get-tuple-element.45.attended_ref, s32[2,128]{1,0:T(2,128)} %bitcast.32, f32[2,128]{1,0:T(2,128)} %bitcast.33), custom_call_target="tpu_custom_call" | custom-call | flops 1073741824 | bytes 1048576 | tf_op jit(solution)/shard_map/pallas_call | solution.py:82
  45.4 0.8 %collective-permute-done.2.far_ref = bf16[64,2304]{1,0:T(8,128)(2,1)S(1)} collective-permute-done((bf16[64,2304]{1,0:T(8,128)(2,1)S(1)}, bf16[64,2304]{1,0:T(8,128)(2,1)S(1)}, u32[]{:S(2)}, u32[]{:S(2)}) %collective-permute-start.2) | collective-permute-done | bytes 294944 | tf_op jit(solution)/shard_map/ppermute | solution.py:663
  46.2 12.8 %shard_map.156 = (f32[64,3072]{1,0:T(8,128)S(1)}, bf16[64,3072]{1,0:T(8,128)(2,1)S(1)}) custom-call(bf16[64,2304]{1,0:T(8,128)(2,1)S(1)} %bitcast.16, bf16[64,2304]{1,0:T(8,128)(2,1)S(1)} %collective-permute-done.2.far_ref, bf16[3072,2048]{1,0:T(8,128)(2,1)} %gate_hbm.1, bf16[3072,2048]{1,0:T(8,128)(2,1)} %up_hbm.1, bf16[2048,3072]{1,0:T(8,128)(2,1)} %down_hbm.1), custom_call_target="tpu_custom_call" | custom-call | flops 4831838208 | bytes 37748736 | tf_op jit(solution)/shard_map/pallas_call | solution.py:82
  59.0 0.2 collective-permute-start.3
  59.2 1.6 %collective-permute-done.3.swapped_ref = bf16[64,3072]{1,0:T(8,128)(2,1)S(1)} collective-permute-done((bf16[64,3072]{1,0:T(8,128)(2,1)S(1)}, bf16[64,3072]{1,0:T(8,128)(2,1)S(1)}, u32[]{:S(2)}, u32[]{:S(2)}) %collective-permute-start.3) | collective-permute-done | bytes 393248 | tf_op jit(solution)/shard_map/ppermute | solution.py:667
  60.8 0.2 shard_map.157
  61.0 13.3 %all_to_all.47 = bf16[8,8,2304]{2,1,0:T(8,128)(2,1)S(1)} all-to-all(bf16[8,8,2304]{2,1,0:T(8,128)(2,1)S(1)} %bitcast.18), channel_id=1, replica_groups={{0,2,4,6,8,10,12,14},{1,3,5,7,9,11,13,15},{16,18,20,22,24,26,28,30},{17..., dimensions={0} | all-to-all | bytes 589824 | tf_op jit(solution)/shard_map/all_to_all | solution.py:613
  74.3 0.8 %shard_map.158 = bf16[8,3072]{1,0:T(8,128)(2,1)} custom-call(bf16[64,2304]{1,0:T(8,128)(2,1)S(1)} %bitcast.17, bf16[16,64]{1,0:T(8,128)(2,1)S(1)} %get-tuple-element.51.main_ref, bf16[3,16,64]{2,1,0:T(8,128)(2,1)S(1)} %get-tuple-element.52.tail_ref, f32[2,8,128]{2,1,0:T(8,128)S(1)} %get-tuple-element.53.gate_ref), custom_call_target="tpu_custom_call" | custom-call | bytes 1048576 | tf_op jit(solution)/shard_map/pallas_call | solution.py:82
Async XLA Ops:
  15.8 1.6 %collective-permute-start = (bf16[64,768]{1,0:T(8,128)(2,1)S(1)}, bf16[64,768]{1,0:T(8,128)(2,1)S(1)}, u32[]{:S(2)}, u32[]{:S(2)}) collective-permute-start(bf16[64,768]{1,0:T(8,128)(2,1)S(1)} %bitcast.21), channel_id=1, source_target_pairs={{0,1},{1,0},{2,3},{3,2},{4,5},{5,4},{6,7},{7,6},{8,9},{9,8},{10,11... | collective-permute-start | bytes 294920 | tf_op jit(solution)/shard_map/ppermute | solution.py:641
  19.0 1.7 %collective-permute-start.1 = (f32[64,896]{1,0:T(8,128)S(1)}, f32[64,896]{1,0:T(8,128)S(1)}, u32[]{:S(2)}, u32[]{:S(2)}) collective-permute-start(f32[64,896]{1,0:T(8,128)S(1)} %get-tuple-element.31), channel_id=1, source_target_pairs={{0,1},{1,0},{2,3},{3,2},{4,5},{5,4},{6,7},{7,6},{8,9},{9,8},{10,11... | collective-permute-start | bytes 688136 | tf_op jit(solution)/shard_map/ppermute | solution.py:657
  44.6 1.6 %collective-permute-start.2 = (bf16[64,2304]{1,0:T(8,128)(2,1)S(1)}, bf16[64,2304]{1,0:T(8,128)(2,1)S(1)}, u32[]{:S(2)}, u32[]{:S(2)}) collective-permute-start(bf16[64,2304]{1,0:T(8,128)(2,1)S(1)} %bitcast.14), channel_id=1, source_target_pairs={{0,1},{1,0},{2,3},{3,2},{4,5},{5,4},{6,7},{7,6},{8,9},{9,8},{10,11... | collective-permute-start | bytes 884744 | tf_op jit(solution)/shard_map/ppermute | solution.py:663
  59.0 1.8 %collective-permute-start.3 = (bf16[64,3072]{1,0:T(8,128)(2,1)S(1)}, bf16[64,3072]{1,0:T(8,128)(2,1)S(1)}, u32[]{:S(2)}, u32[]{:S(2)}) collective-permute-start(bf16[64,3072]{1,0:T(8,128)(2,1)S(1)} %get-tuple-element.50), channel_id=1, source_target_pairs={{0,1},{1,0},{2,3},{3,2},{4,5},{5,4},{6,7},{7,6},{8,9},{9,8},{10,11... | collective-permute-start | bytes 1179656 | tf_op jit(solution)/shard_map/ppermute | solution.py:667

commit v6 on v5

--- a/solution.py
+++ b/solution.py
@@ -595,9 +595,10 @@
         last = jnp.zeros((2 * rows, PIECE), F32)
         for n in range(BLOCKS):
             cols = pl.ds(n * PIECE, PIECE)
-            found = dot(main_ref[...], part_ref[:, cols])
-            out_ref[:, cols] = (found[:rows] * first + found[rows:] * second).astype(BF16)
-            last += dot(tail_ref[n], part_ref[:, cols])
+            both = jnp.concatenate([main_ref[...], tail_ref[n]], axis=0)
+            found = dot(both, part_ref[:, cols])
+            out_ref[:, cols] = (found[:rows] * first + found[rows : 2 * rows] * second).astype(BF16)
+            last += found[2 * rows :]
         cols = pl.ds(BLOCKS * PIECE, PIECE)
         out_ref[:, cols] = (last[:rows] * first + last[rows:] * second).astype(BF16)
 

time: 75.5 us -> 75.5 us (level)
  no operation moved by 1% of the time
where the time goes in v6:
time: 75.5 us; the launch traced here: 75.1 us
  blocking collectives  50.2 us (66%)
  Pallas kernels  21.1 us (28%)
  waiting for transfers between devices  2.37 us (3%)
  starting transfers between devices  0.78 us (1%)
    all_to_all x4, blocking collectives, exchange(): return lax.all_to_all(x, 'wide', 0, 0, tiled=True, axis_index_groups=groups)  50.2 us
    pallas_call x10, Pallas kernels, call(): pl.pallas_call(kernel, out_shape=outs, in_specs=specs, out_specs=out_spec...  21.1 us
    ppermute x1, waiting for transfers between devices, local(): swapped = lax.ppermute(theirs, 'wide', siblings)  1.59 us
  transfers between devices with their start and end apart: 4, of which 2 were waited for; matrix products, arithmetic and copies ran while one was open for 0% of the time, Pallas kernels for 5%

profile of v6, /device:TPU:0, one launch (start us, length us, event | category | flops | bytes accessed | tf_op | source)
XLA Modules:
  0.0 75.1 jit_solution(6790362755376121036)
XLA Ops:
  0.6 1.0 %shard_map.149 = bf16[64,768]{1,0:T(8,128)(2,1)S(1)} custom-call(bf16[8,3072]{1,0:T(8,128)(2,1)} %refs_8_.1, s32[128]{0:T(128)} %bitcast.26), custom_call_target="tpu_custom_call" | custom-call | bytes 1048576 | tf_op jit(solution)/shard_map/pallas_call | solution.py:82
  1.6 14.2 %all_to_all.44 = bf16[8,8,768]{2,1,0:T(8,128)(2,1)S(1)} all-to-all(bf16[8,8,768]{2,1,0:T(8,128)(2,1)S(1)} %bitcast.24), channel_id=1, replica_groups={{0,2,4,6,8,10,12,14},{1,3,5,7,9,11,13,15},{16,18,20,22,24,26,28,30},{17..., dimensions={0} | all-to-all | bytes 196608 | tf_op jit(solution)/shard_map/all_to_all | solution.py:614
  15.8 0.0 collective-permute-start
  15.8 1.6 %shard_map.150 = (bf16[512,512]{1,0:T(8,128)(2,1)S(1)}, bf16[512,512]{1,0:T(8,128)(2,1)S(1)}, bf16[512,512]{1,0:T(8,128)(2,1)S(1)}, bf16[512,512]{1,0:T(8,128)(2...) custom-call(bf16[64,768]{1,0:T(8,128)(2,1)S(1)} %bitcast.22, ...), custom_call_target="tpu_custom_call" | custom-call | flops 1073741824 | bytes 1048576 | tf_op jit(solution)/shard_map/pallas_call | solution.py:82
  17.5 0.0 collective-permute-done.far_ref
  17.5 1.5 %shard_map.151 = (f32[64,896]{1,0:T(8,128)S(1)}, f32[64,896]{1,0:T(8,128)S(1)}) custom-call(bf16[64,768]{1,0:T(8,128)(2,1)S(1)} %bitcast.23, bf16[64,768]{1,0:T(8,128)(2,1)S(1)} %collective-permute-done.far_ref, bf16[512,512]{1,0:T(8,128)(2,1)S(1)} %get-tuple-element.28.key_ref, bf16[512,512]{1,0:T(8,128)(2,1)S(1)} %get-tuple-element.29.value_ref), custom_call_target="tpu_custom_call" | custom-call | bytes 1048576 | tf_op jit(solution)/shard_map/pallas_call | solution.py:82
  19.0 0.6 collective-permute-start.1
  19.6 1.1 %shard_map.152 = (f32[32,768]{1,0:T(8,128)S(1)}, f32[32,128]{1,0:T(8,128)S(1)}) custom-call(f32[64,896]{1,0:T(8,128)S(1)} %get-tuple-element.30._.kept_ref, bf16[8,3072]{1,0:T(8,128)(2,1)S(1)} %get-tuple-element.32.query_ref, bf16[512,512]{1,0:T(8,128)(2,1)S(1)} %get-tuple-element.33.key_ref, bf16[512,512]{1,0:T(8,128)(2,1)S(1)} %get-tuple-element.34.value_ref, ...), custom_call_target="tpu_custom_call" | custom-call | flops 1073741824 | bytes 1048576 | tf_op jit(solution)/shard_map/pallas_call | solution.py:82
  20.7 0.0 collective-permute-done.1.swapped_ref
  20.7 0.5 shard_map.153
  21.2 9.9 %all_to_all.45 = bf16[8,8,896]{2,1,0:T(8,128)(2,1)S(1)} all-to-all(bf16[8,8,896]{2,1,0:T(8,128)(2,1)S(1)} %bitcast.20), channel_id=1, replica_groups={{0,2,4,6,8,10,12,14},{1,3,5,7,9,11,13,15},{16,18,20,22,24,26,28,30},{17..., dimensions={0} | all-to-all | bytes 229376 | tf_op jit(solution)/shard_map/all_to_all | solution.py:614
  31.1 0.7 shard_map.154
  31.9 12.7 %all_to_all.46 = bf16[8,8,2304]{2,1,0:T(8,128)(2,1)S(1)} all-to-all(bf16[8,8,2304]{2,1,0:T(8,128)(2,1)S(1)} %bitcast.25), channel_id=1, replica_groups={{0,2,4,6,8,10,12,14},{1,3,5,7,9,11,13,15},{16,18,20,22,24,26,28,30},{17..., dimensions={0} | all-to-all | bytes 589824 | tf_op jit(solution)/shard_map/all_to_all | solution.py:614
  44.6 0.0 collective-permute-start.2
  44.6 0.8 %shard_map.155 = (bf16[8,3072]{1,0:T(8,128)(2,1)}, bf16[16,64]{1,0:T(8,128)(2,1)S(1)}, bf16[3,16,64]{2,1,0:T(8,128)(2,1)S(1)}, f32[2,8,128]{2,1,0:T(8,128)S(1)}) custom-call(bf16[64,2304]{1,0:T(8,128)(2,1)S(1)} %bitcast.15, bf16[8,3072]{1,0:T(8,128)(2,1)S(1)} %get-tuple-element.45.attended_ref, s32[2,128]{1,0:T(2,128)} %bitcast.32, f32[2,128]{1,0:T(2,128)} %bitcast.33), custom_call_target="tpu_custom_call" | custom-call | flops 1073741824 | bytes 1048576 | tf_op jit(solution)/shard_map/pallas_call | solution.py:82
  45.4 0.8 %collective-permute-done.2.far_ref = bf16[64,2304]{1,0:T(8,128)(2,1)S(1)} collective-permute-done((bf16[64,2304]{1,0:T(8,128)(2,1)S(1)}, bf16[64,2304]{1,0:T(8,128)(2,1)S(1)}, u32[]{:S(2)}, u32[]{:S(2)}) %collective-permute-start.2) | collective-permute-done | bytes 294944 | tf_op jit(solution)/shard_map/ppermute | solution.py:664
  46.2 12.8 %shard_map.156 = (f32[64,3072]{1,0:T(8,128)S(1)}, bf16[64,3072]{1,0:T(8,128)(2,1)S(1)}) custom-call(bf16[64,2304]{1,0:T(8,128)(2,1)S(1)} %bitcast.16, bf16[64,2304]{1,0:T(8,128)(2,1)S(1)} %collective-permute-done.2.far_ref, bf16[3072,2048]{1,0:T(8,128)(2,1)} %gate_hbm.1, bf16[3072,2048]{1,0:T(8,128)(2,1)} %up_hbm.1, bf16[2048,3072]{1,0:T(8,128)(2,1)} %down_hbm.1), custom_call_target="tpu_custom_call" | custom-call | flops 4831838208 | bytes 37748736 | tf_op jit(solution)/shard_map/pallas_call | solution.py:82
  59.0 0.2 collective-permute-start.3
  59.2 1.6 %collective-permute-done.3.swapped_ref = bf16[64,3072]{1,0:T(8,128)(2,1)S(1)} collective-permute-done((bf16[64,3072]{1,0:T(8,128)(2,1)S(1)}, bf16[64,3072]{1,0:T(8,128)(2,1)S(1)}, u32[]{:S(2)}, u32[]{:S(2)}) %collective-permute-start.3) | collective-permute-done | bytes 393248 | tf_op jit(solution)/shard_map/ppermute | solution.py:668
  60.8 0.2 shard_map.157
  61.0 13.3 %all_to_all.47 = bf16[8,8,2304]{2,1,0:T(8,128)(2,1)S(1)} all-to-all(bf16[8,8,2304]{2,1,0:T(8,128)(2,1)S(1)} %bitcast.18), channel_id=1, replica_groups={{0,2,4,6,8,10,12,14},{1,3,5,7,9,11,13,15},{16,18,20,22,24,26,28,30},{17..., dimensions={0} | all-to-all | bytes 589824 | tf_op jit(solution)/shard_map/all_to_all | solution.py:614
  74.3 0.8 %shard_map.158 = bf16[8,3072]{1,0:T(8,128)(2,1)} custom-call(bf16[64,2304]{1,0:T(8,128)(2,1)S(1)} %bitcast.17, bf16[16,64]{1,0:T(8,128)(2,1)S(1)} %get-tuple-element.51.main_ref, bf16[3,16,64]{2,1,0:T(8,128)(2,1)S(1)} %get-tuple-element.52.tail_ref, f32[2,8,128]{2,1,0:T(8,128)S(1)} %get-tuple-element.53.gate_ref), custom_call_target="tpu_custom_call" | custom-call | bytes 1048576 | tf_op jit(solution)/shard_map/pallas_call | solution.py:82
Async XLA Ops:
  15.8 1.6 %collective-permute-start = (bf16[64,768]{1,0:T(8,128)(2,1)S(1)}, bf16[64,768]{1,0:T(8,128)(2,1)S(1)}, u32[]{:S(2)}, u32[]{:S(2)}) collective-permute-start(bf16[64,768]{1,0:T(8,128)(2,1)S(1)} %bitcast.21), channel_id=1, source_target_pairs={{0,1},{1,0},{2,3},{3,2},{4,5},{5,4},{6,7},{7,6},{8,9},{9,8},{10,11... | collective-permute-start | bytes 294920 | tf_op jit(solution)/shard_map/ppermute | solution.py:642
  19.0 1.7 %collective-permute-start.1 = (f32[64,896]{1,0:T(8,128)S(1)}, f32[64,896]{1,0:T(8,128)S(1)}, u32[]{:S(2)}, u32[]{:S(2)}) collective-permute-start(f32[64,896]{1,0:T(8,128)S(1)} %get-tuple-element.31), channel_id=1, source_target_pairs={{0,1},{1,0},{2,3},{3,2},{4,5},{5,4},{6,7},{7,6},{8,9},{9,8},{10,11... | collective-permute-start | bytes 688136 | tf_op jit(solution)/shard_map/ppermute | solution.py:658
  44.6 1.6 %collective-permute-start.2 = (bf16[64,2304]{1,0:T(8,128)(2,1)S(1)}, bf16[64,2304]{1,0:T(8,128)(2,1)S(1)}, u32[]{:S(2)}, u32[]{:S(2)}) collective-permute-start(bf16[64,2304]{1,0:T(8,128)(2,1)S(1)} %bitcast.14), channel_id=1, source_target_pairs={{0,1},{1,0},{2,3},{3,2},{4,5},{5,4},{6,7},{7,6},{8,9},{9,8},{10,11... | collective-permute-start | bytes 884744 | tf_op jit(solution)/shard_map/ppermute | solution.py:664
  59.0 1.8 %collective-permute-start.3 = (bf16[64,3072]{1,0:T(8,128)(2,1)S(1)}, bf16[64,3072]{1,0:T(8,128)(2,1)S(1)}, u32[]{:S(2)}, u32[]{:S(2)}) collective-permute-start(bf16[64,3072]{1,0:T(8,128)(2,1)S(1)} %get-tuple-element.50), channel_id=1, source_target_pairs={{0,1},{1,0},{2,3},{3,2},{4,5},{5,4},{6,7},{7,6},{8,9},{9,8},{10,11... | collective-permute-start | bytes 1179656 | tf_op jit(solution)/shard_map/ppermute | solution.py:668
